TPU v7x, 8 devices: a whole 2x2x1 slice. The times are simulated.
8 devices in a mesh: col: 2 (over z, y), row: 2 (over x), depth: 2 (over core).
Axes of the slice: x: 2, y: 2, z: 1, core: 2. Of those that a mesh axis runs over, the one named last changes fastest.
Arguments:
- a_mat: bfloat16 [8192, 16384], P(('depth', 'row', 'col'))
- b_mat: bfloat16 [16384, 10240], P(('depth', 'row', 'col'))
Outputs:
- output: bfloat16 [8192, 10240], P(('depth', 'row', 'col'))
All inputs are finite; a program needn't handle non-finite values.
Results may differ from a plain program's by a relative error of at most 0.001.
Values are sent between devices in bfloat16 or wider.
A program may use at most 1 GiB of HBM per device.

v0:
```python
import jax
import jax.numpy as jnp
from jax import lax
from jax.sharding import PartitionSpec as P


def solution(mesh):
    all_axes = ("depth", "row", "col")
    depth_size = mesh.shape["depth"]
    col_size = mesh.shape["col"]

    def device_block(a_rows, b_rows):
        a_part = lax.all_to_all(a_rows, "depth", 1, 0, tiled=True)
        a_block = lax.all_gather(a_part, "col", axis=0, tiled=True)
        b_part = lax.all_to_all(b_rows, "col", 1, 0, tiled=True)
        b_block = lax.all_gather(b_part, "row", axis=0, tiled=True)
        part_sum = jnp.dot(a_block, b_block, preferred_element_type=jnp.float32)
        rows_dev = a_rows.shape[0]
        n_cols = part_sum.shape[1]
        grouped = part_sum.reshape(col_size, depth_size * rows_dev, n_cols)
        summed = lax.psum_scatter(grouped, "depth", scatter_dimension=1, tiled=True)
        rounded = summed.astype(jnp.bfloat16).reshape(col_size * rows_dev, n_cols)
        return lax.all_to_all(rounded, "col", 0, 1, tiled=True)

    return jax.shard_map(device_block, mesh=mesh, in_specs=(P(all_axes, None), P(all_axes, None)), out_specs=P(all_axes, None), check_vma=False)
```

profile of v0, /device:TPU:0, one launch (start us, length us, event | category | flops | bytes accessed | tf_op | source)
XLA Modules:
  0.0 3025.6 jit_solution(696094797498020265)
XLA Ops:
  6.5 0.0 all-gather.3.cloned.1.call-start
  6.5 44.0 %copy.5 = bf16[1024,16384]{0,1:T(8,128)(2,1)} copy(bf16[1024,16384]{1,0:T(8,128)(2,1)} %param.2) | data formatting | bytes 67108864 | tf_op args[0]
  50.6 58.0 %all_to_all.54 = bf16[1024,2,8192]{0,2,1:T(8,128)(2,1)} all-to-all(bf16[1024,2,8192]{0,2,1:T(8,128)(2,1)} %bitcast.17), channel_id=1, replica_groups=mesh['col'=2,'row'=2,'depth'=2] {'depth'}, dimensions={1} | all-to-all | bytes 67108864 | tf_op jit(solution)/shard_map/all_to_all | solution.py:13
  108.6 40.6 %copy.6 = bf16[2,1024,8192]{2,1,0:T(8,128)(2,1)} copy(bf16[2,1024,8192]{1,2,0:T(8,128)(2,1)} %bitcast.16) | data formatting | bytes 67108864 | tf_op jit(solution)/shard_map/all_to_all | solution.py:13
  149.1 0.0 all-gather.3.cloned.1.call-update
  149.1 0.0 all-gather.5.cloned.1.call-start
  149.2 54.7 %copy.7 = bf16[2048,10240]{0,1:T(8,128)(2,1)} copy(bf16[2048,10240]{1,0:T(8,128)(2,1)} %param.3) | data formatting | bytes 83886080 | tf_op args[1]
  203.9 942.8 %all_to_all.55 = bf16[2048,2,5120]{0,2,1:T(8,128)(2,1)} all-to-all(bf16[2048,2,5120]{0,2,1:T(8,128)(2,1)} %bitcast.14), channel_id=1, replica_groups=mesh['col'=2,'row'=2,'depth'=2] {'col'}, dimensions={1} | all-to-all | bytes 83886080 | tf_op jit(solution)/shard_map/all_to_all | solution.py:15
  1146.7 50.5 %copy.8 = bf16[2,2048,5120]{2,1,0:T(8,128)(2,1)} copy(bf16[2,2048,5120]{1,2,0:T(8,128)(2,1)} %bitcast.13) | data formatting | bytes 83886080 | tf_op jit(solution)/shard_map/all_to_all | solution.py:15
  1197.2 0.0 all-gather.5.cloned.1.call-update
  1197.2 0.0 reduce-scatter.2.cloned.1.call-start
  1197.3 167.1 %all-gather.3.cloned.1.call-done = bf16[4096,8192]{1,0:T(8,128)(2,1)} async-done(((bf16[2048,8192]{1,0:T(8,128)(2,1)}), bf16[4096,8192]{1,0:T(8,128)(2,1)}) %all-gather.3.cloned.1.call-update) | async-done | bytes 67108880 | tf_op jit(solution)/shard_map/all_gather | solution.py:14
  1364.4 953.5 %all-gather.5.cloned.1.call-done = bf16[8192,5120]{1,0:T(8,128)(2,1)} async-done(((bf16[4096,5120]{1,0:T(8,128)(2,1)}), bf16[8192,5120]{1,0:T(8,128)(2,1)}) %all-gather.5.cloned.1.call-update) | async-done | bytes 83886096 | tf_op jit(solution)/shard_map/all_gather | solution.py:16
  2317.9 362.8 %fusion = f32[4096,5120]{1,0:T(8,128)} fusion(bf16[4096,8192]{1,0:T(8,128)(2,1)} %all-gather.3.cloned.1.call-done, bf16[8192,5120]{1,0:T(8,128)(2,1)} %all-gather.5.cloned.1.call-done), kind=kOutput, calls=%fused_computation | convolution fusion | flops 343597383680 | bytes 234881024 | tf_op jit(solution)/shard_map/dot_general | solution.py:17
  2680.7 0.0 reduce-scatter.2.cloned.1.call-update
  2680.7 84.2 %reduce-scatter.2.cloned.1.call-done = f32[2,1024,5120]{2,1,0:T(8,128)} async-done(((f32[2,2048,5120]{2,1,0:T(8,128)}), f32[2,1024,5120]{2,1,0:T(8,128)}) %reduce-scatter.2.cloned.1.call-update) | async-done | bytes 41943056 | tf_op jit(solution)/shard_map/reduce_scatter | solution.py:21
  2764.9 14.9 convert_element_type.3
  2779.8 232.0 %all_to_all.56 = bf16[2,1024,5120]{2,1,0:T(8,128)(2,1)S(1)} all-to-all(bf16[2,1024,5120]{2,1,0:T(8,128)(2,1)S(1)} %convert_element_type.3), channel_id=1, replica_groups=mesh['col'=2,'row'=2,'depth'=2] {'col'}, dimensions={0} | all-to-all | bytes 41943040 | tf_op jit(solution)/shard_map/all_to_all | solution.py:23
  3011.8 7.3 copy.10
Async XLA Ops:
  6.5 1357.8 %all-gather.3.cloned.1.call-start = ((), (), s32[]{:S(2)}) async-start(), calls=%async_computation.4 | async-start | bytes 100663296 | tf_op jit(solution)/shard_map/all_gather | solution.py:14
  149.1 2168.8 %all-gather.5.cloned.1.call-start = ((), (), s32[]{:S(2)}) async-start(), calls=%async_computation.5 | async-start | bytes 125829120 | tf_op jit(solution)/shard_map/all_gather | solution.py:16
  1197.2 1567.7 %reduce-scatter.2.cloned.1.call-start = ((), (), s32[]{:S(2)}) async-start(), calls=%async_computation.6 | async-start | bytes 125829120 | tf_op jit(solution)/shard_map/reduce_scatter | solution.py:21
Sparse Core Ops, SparseCore 0:
  149.3 1215.0 all-gather.2
  1365.9 951.9 all-gather.4
  2680.8 84.0 reduce-scatter.1
where the time goes:
time: 3030 us
  blocking collectives  1230 us (41%)
  waiting for transfers between devices  1200 us (40%)
  matrix products  363 us (12%)
  local copies, waits for them, and re-layouts  197 us (7%)
    all_gather x1, waiting for transfers between devices, device_block(): b_block = lax.all_gather(b_part, 'row', axis=0, tiled=True)  954 us
    all_to_all x1, blocking collectives, device_block(): b_part = lax.all_to_all(b_rows, 'col', 1, 0, tiled=True)  943 us
    dot_general x1, matrix products, device_block(): part_sum = jnp.dot(a_block, b_block, preferred_element_type=jnp.float32)  363 us
    all_to_all x1, blocking collectives, device_block(): return lax.all_to_all(rounded, 'col', 0, 1, tiled=True)  232 us
    all_gather x1, waiting for transfers between devices, device_block(): a_block = lax.all_gather(a_part, 'col', axis=0, tiled=True)  167 us
    unnamed x2, local copies, waits for them, and re-layouts  98.7 us
    reduce_scatter x1, waiting for transfers between devices, device_block(): summed = lax.psum_scatter(grouped, 'depth', scatter_dimension=1, tiled=True)  84.2 us
  transfers between devices with their start and end apart: 3, of which 3 were waited for; matrix products, arithmetic and copies ran while one was open for 3% of the time, Pallas kernels for 0%

commit v1 on v0

v1 whole, which is shorter than its diff:
```python
import functools

import jax
import jax.numpy as jnp
from jax import lax
from jax.experimental import pallas as pl
from jax.experimental.pallas import tpu as pltpu
from jax.sharding import PartitionSpec as P

MESH = pl.DeviceIdType.MESH
BLOCK = 512
TILES = 4
AHEAD = 4
SLOTS = 2


def kernel(
    n_blocks, tile, a_ref, b_ref, c_ref, b_got, r_got,
    a_buf, b_buf, p_buf, q_buf, r_buf, c_buf,
    a_own_sem, a_send, a_recv, b_send, b_recv, b_load_sem, p_send, r_recv, r_load_sem, c_sem,
):
    col, row, core = lax.axis_index("col"), lax.axis_index("row"), lax.axis_index("depth")
    neighbour, partner, sibling = {"col": 1 - col}, {"row": 1 - row}, {"depth": 1 - core}
    depth, block = b_ref.shape[0], b_buf.shape[2]

    def rows_of(m):
        return pl.ds(pl.multiple_of(m * tile, tile), tile)

    def cols_of(t):
        return pl.ds(pl.multiple_of(t * block, block), block)

    def a_cols(h, r):
        return pl.ds(pl.multiple_of((h * 4 + r * 2) * depth, depth), 2 * depth)

    def a_half(h):
        return pl.ds(h * 2 * depth, 2 * depth)

    def own_a(h):
        return pltpu.make_async_copy(a_ref.at[:, a_cols(h, row)], a_buf.at[0, :, a_half(h)], a_own_sem.at[h])

    def send_a(m, h):
        return pltpu.make_async_remote_copy(
            src_ref=a_ref.at[rows_of(m), a_cols(h, 1 - row)], dst_ref=a_buf.at[1, rows_of(m), a_half(h)],
            send_sem=a_send.at[m, h], recv_sem=a_recv.at[m, h], device_id=partner, device_id_type=MESH)

    def send_b(way, t):
        return pltpu.make_async_remote_copy(
            src_ref=b_got.at[0, t] if way == 2 else b_ref.at[:, cols_of(t)], dst_ref=b_got.at[way, t],
            send_sem=b_send.at[way, t], recv_sem=b_recv.at[way, t],
            device_id=neighbour if way == 0 else sibling, device_id_type=MESH)

    def load_b(t, slot):
        places = (core * 2 + col, core * 2 + 1 - col, (1 - core) * 2 + col, (1 - core) * 2 + 1 - col)
        return [
            pltpu.make_async_copy(
                b_ref.at[:, cols_of(t)] if i == 0 else b_got.at[i - 1, t],
                b_buf.at[slot, pl.ds(pl.multiple_of(place * depth, depth), depth), :], b_load_sem.at[slot, i])
            for i, place in enumerate(places)
        ]

    def send_p(s, m):
        return pltpu.make_async_remote_copy(
            src_ref=p_buf.at[lax.rem(s, SLOTS), rows_of(m)], dst_ref=r_got.at[s, rows_of(m)],
            send_sem=p_send.at[s, m], recv_sem=r_recv.at[s, m], device_id=partner, device_id_type=MESH)

    def load_r(q, m):
        return pltpu.make_async_copy(r_got.at[q, rows_of(m)], r_buf.at[m], r_load_sem.at[m])

    def store_c(q, m):
        return pltpu.make_async_copy(c_buf.at[m], c_ref.at[rows_of(m), cols_of(q)], c_sem.at[m])

    def product(whose, m, slot):
        return jnp.dot(a_buf[whose, rows_of(m), :], b_buf[slot], preferred_element_type=jnp.float32)

    def pass_on(t):
        send_b(0, t).wait_recv()
        send_b(2, t).start()
        send_b(1, t).start()

        @pl.when(t + AHEAD < n_blocks)
        def _():
            send_b(0, t + AHEAD).start()

    def start_load_first(t):
        send_b(1, t).wait_recv()
        send_b(2, t).wait_recv()
        for copy in load_b(t, 0):
            copy.start()

    barrier = pltpu.get_barrier_semaphore()
    for other in (neighbour, partner, sibling):
        pl.semaphore_signal(barrier, inc=1, device_id=other, device_id_type=MESH)
    pl.semaphore_wait(barrier, 3)

    for m in range(TILES):
        for h in range(2):
            send_a(m, h).start()
        if m == 0:
            for t in range(AHEAD):
                send_b(0, t).start()
    for h in range(2):
        own_a(h).start()

    @pl.loop(0, AHEAD)
    def _(t):
        pass_on(t)

    start_load_first(0)
    for h in range(2):
        own_a(h).wait()
    for copy in load_b(0, 0):
        copy.wait()

    @pl.loop(0, n_blocks + SLOTS)
    def _(s):
        @pl.when(s < n_blocks)
        def _():
            @pl.when(s > 0)
            def _():
                for copy in load_b(s, 0):
                    copy.wait()

            @pl.loop(0, TILES)
            def _(m):
                @pl.when(s == 0)
                def _():
                    for h in range(2):
                        send_a(m, h).wait_recv()

                @pl.when(s >= SLOTS)
                def _():
                    send_p(s - SLOTS, m).wait_send()

                p_buf[lax.rem(s, SLOTS), rows_of(m), :] = product(1, m, 0)
                send_p(s, m).start()

            @pl.when(s + AHEAD < n_blocks)
            def _():
                pass_on(s + AHEAD)

            @pl.when(s + 1 < n_blocks)
            def _():
                start_load_first(s + 1)

        @pl.when(s >= SLOTS)
        def _():
            q = s - SLOTS
            for copy in load_b(q, 1):
                copy.wait()

            @pl.loop(0, TILES)
            def _(m):
                q_buf[m] = product(0, m, 1)

            @pl.when(q + 1 < n_blocks)
            def _():
                for copy in load_b(q + 1, 1):
                    copy.start()

            @pl.loop(0, TILES)
            def _(m):
                send_p(q, m).wait_recv()
                load_r(q, m).start()
                load_r(q, m).wait()

                @pl.when(q > 0)
                def _():
                    store_c(q - 1, m).wait()

                c_buf[m] = (q_buf[m] + r_buf[m]).astype(c_buf.dtype)
                store_c(q, m).start()

        @pl.when(s == SLOTS - 1)
        def _():
            for copy in load_b(0, 1):
                copy.start()

    for m in range(TILES):
        store_c(n_blocks - 1, m).wait()
        for h in range(2):
            send_a(m, h).wait_send()

    @pl.loop(n_blocks - SLOTS, n_blocks)
    def _(s):
        for m in range(TILES):
            send_p(s, m).wait_send()

    @pl.loop(0, n_blocks)
    def _(t):
        for way in range(3):
            send_b(way, t).wait_send()


def device_product(block, a_rows, b_rows):
    rows, _ = a_rows.shape
    depth, n_cols = b_rows.shape
    n_blocks, tile = n_cols // block, rows // TILES
    anywhere = pl.BlockSpec(memory_space=pl.ANY)
    dma = pltpu.SemaphoreType.DMA
    c_rows, _, _ = pl.pallas_call(
        functools.partial(kernel, n_blocks, tile),
        out_shape=(
            jax.ShapeDtypeStruct((rows, n_cols), jnp.bfloat16),
            jax.ShapeDtypeStruct((3, n_blocks, depth, block), jnp.bfloat16),
            jax.ShapeDtypeStruct((n_blocks, rows, block), jnp.float32),
        ),
        in_specs=[anywhere] * 2,
        out_specs=(anywhere,) * 3,
        scratch_shapes=[
            pltpu.VMEM((2, rows, 4 * depth), jnp.bfloat16),
            pltpu.VMEM((2, 4 * depth, block), jnp.bfloat16),
            pltpu.VMEM((SLOTS, rows, block), jnp.float32),
            pltpu.VMEM((TILES, tile, block), jnp.float32),
            pltpu.VMEM((TILES, tile, block), jnp.float32),
            pltpu.VMEM((TILES, tile, block), jnp.bfloat16),
            dma((2,)),
            dma((TILES, 2)),
            dma((TILES, 2)),
            dma((3, n_blocks)),
            dma((3, n_blocks)),
            dma((2, 4)),
            dma((n_blocks, TILES)),
            dma((n_blocks, TILES)),
            dma((TILES,)),
            dma((TILES,)),
        ],
        compiler_params=pltpu.CompilerParams(
            collective_id=0, has_side_effects=True, vmem_limit_bytes=66_000_000
        ),
        name="split_sum_product",
    )(a_rows, b_rows)
    return c_rows


def solution(mesh, block=BLOCK):
    all_axes = ("depth", "row", "col")
    return jax.shard_map(
        functools.partial(device_product, block),
        mesh=mesh,
        in_specs=(P(all_axes, None), P(all_axes, None)),
        out_specs=P(all_axes, None),
        check_vma=False,
    )
```

time: 3030 us -> 1290 us (0.43)
  Pallas kernels: 0 us -> 1270 us
  blocking collectives: 1230 us -> 0 us
  waiting for transfers between devices: 1200 us -> 0 us
  matrix products: 363 us -> 0 us
  local copies, waits for them, and re-layouts: 197 us -> 17.6 us
    pallas_call x0 -> x1, Pallas kernels: none -> 1270 us  [device_product(): pl.pallas_call(functools.partial(kernel, n_blocks, tile), out_shape=(jax....]
    all_to_all x3 -> x0, blocking collectives: 1230 us -> none  [the longest x1 943 us: device_block(): b_part = lax.all_to_all(b_rows, 'col', 1, 0, tiled=True)]
    all_gather x2 -> x0, waiting for transfers between devices: 1120 us -> none  [the longest x1 954 us: device_block(): b_block = lax.all_gather(b_part, 'row', axis=0, tiled=True)]
    dot_general x1 -> x0, matrix products: 363 us -> none  [device_block(): part_sum = jnp.dot(a_block, b_block, preferred_element_type=jnp.float32)]
    all_to_all x3 -> x0, local copies, waits for them, and re-layouts: 98.3 us -> none  [the longest x1 50.5 us: device_block(): b_part = lax.all_to_all(b_rows, 'col', 1, 0, tiled=True)]
    reduce_scatter x1 -> x0, waiting for transfers between devices: 84.2 us -> none  [device_block(): summed = lax.psum_scatter(grouped, 'depth', scatter_dimension=1, tiled=True)]
    unnamed x2 -> x1, local copies, waits for them, and re-layouts: 98.7 us -> 17.6 us
  transfers between devices with their start and end apart: 3 -> 0, of which waited for: 3 -> 0; matrix products, arithmetic and copies ran while one was open for 3% -> 0% of each run, Pallas kernels for 0% -> 0%
where the time goes in v1:
time: 1290 us
  Pallas kernels  1270 us (98%)
  local copies, waits for them, and re-layouts  17.6 us (1%)
    pallas_call x1, Pallas kernels, device_product(): pl.pallas_call(functools.partial(kernel, n_blocks, tile), out_shape=(jax....  1270 us

profile of v1, /device:TPU:0, one launch (start us, length us, event | category | flops | bytes accessed | tf_op | source)
XLA Modules:
  0.0 1286.0 jit_solution(14847861685544108908)
XLA Ops:
  0.0 1268.4 %split_sum_product.1 = (bf16[1024,10240]{1,0:T(8,128)(2,1)}, bf16[3,20,2048,512]{3,2,1,0:T(8,128)(2,1)}, f32[20,1024,512]{2,1,0:T(8,128)}) custom-call(bf16[1024,16384]{1,0:T(8,128)(2,1)} %a_ref.1, bf16[2048,10240]{1,0:T(8,128)(2,1)} %b_ref.1), custom_call_target="tpu_custom_call" | custom-call | tf_op jit(solution)/shard_map/split_sum_product/pallas_call | solution.py:200
  1268.4 17.6 %copy.4 = bf16[1024,10240]{1,0:T(8,128)(2,1)} copy(bf16[1024,10240]{1,0:T(8,128)(2,1)} %get-tuple-element.6) | data formatting | bytes 41943040

commit v2 on v1

--- a/solution.py
+++ b/solution.py
@@ -7,18 +7,21 @@
 from jax.experimental.pallas import tpu as pltpu
 from jax.sharding import PartitionSpec as P
 
+
 MESH = pl.DeviceIdType.MESH
 BLOCK = 512
 TILES = 4
 AHEAD = 4
-SLOTS = 2
+SLOTS = 3
+LATE = 128
 
 
 def kernel(
-    n_blocks, tile, a_ref, b_ref, c_ref, b_got, r_got,
+    n_blocks, tile, a_ref, b_ref, c_ref, r_got, p_early, p_late, q_last, b_got,
     a_buf, b_buf, p_buf, q_buf, r_buf, c_buf,
-    a_own_sem, a_send, a_recv, b_send, b_recv, b_load_sem, p_send, r_recv, r_load_sem, c_sem,
+    a_own_sem, a_send, a_recv, b_send, b_recv, b_load_sem, p_send, r_recv, r_load_sem, c_sem, q_sem, last_sem,
 ):
+    last = n_blocks - 1
     col, row, core = lax.axis_index("col"), lax.axis_index("row"), lax.axis_index("depth")
     neighbour, partner, sibling = {"col": 1 - col}, {"row": 1 - row}, {"depth": 1 - core}
     depth, block = b_ref.shape[0], b_buf.shape[2]
@@ -69,6 +72,17 @@
     def store_c(q, m):
         return pltpu.make_async_copy(c_buf.at[m], c_ref.at[rows_of(m), cols_of(q)], c_sem.at[m])
 
+    def store_q(q, m):
+        return pltpu.make_async_copy(q_buf.at[m], q_last.at[q - last + 1, rows_of(m)], q_sem.at[m])
+
+    def store_p(m):
+        early = p_early.shape[1]
+        return [
+            pltpu.make_async_copy(
+                p_buf.at[last % SLOTS, rows_of(m), pl.ds(start, out.shape[1])], out.at[rows_of(m)], last_sem.at[i, m])
+            for i, (start, out) in enumerate(((0, p_early), (early, p_late)))
+        ]
+
     def product(whose, m, slot):
         return jnp.dot(a_buf[whose, rows_of(m), :], b_buf[slot], preferred_element_type=jnp.float32)
 
@@ -132,7 +146,15 @@
                     send_p(s - SLOTS, m).wait_send()
 
                 p_buf[lax.rem(s, SLOTS), rows_of(m), :] = product(1, m, 0)
-                send_p(s, m).start()
+
+                @pl.when(s < last)
+                def _():
+                    send_p(s, m).start()
+
+                @pl.when(s == last)
+                def _():
+                    for copy in store_p(m):
+                        copy.start()
 
             @pl.when(s + AHEAD < n_blocks)
             def _():
@@ -150,62 +172,92 @@
 
             @pl.loop(0, TILES)
             def _(m):
+                @pl.when(q == last)
+                def _():
+                    store_q(q - 1, m).wait()
+
                 q_buf[m] = product(0, m, 1)
+
+                @pl.when(q >= last - 1)
+                def _():
+                    store_q(q, m).start()
 
             @pl.when(q + 1 < n_blocks)
             def _():
                 for copy in load_b(q + 1, 1):
                     copy.start()
 
-            @pl.loop(0, TILES)
-            def _(m):
-                send_p(q, m).wait_recv()
-                load_r(q, m).start()
-                load_r(q, m).wait()
-
-                @pl.when(q > 0)
-                def _():
-                    store_c(q - 1, m).wait()
-
-                c_buf[m] = (q_buf[m] + r_buf[m]).astype(c_buf.dtype)
-                store_c(q, m).start()
+            @pl.when(q < last - 1)
+            def _():
+                @pl.loop(0, TILES)
+                def _(m):
+                    send_p(q, m).wait_recv()
+                    load_r(q, m).start()
+                    load_r(q, m).wait()
+
+                    @pl.when(q > 0)
+                    def _():
+                        store_c(q - 1, m).wait()
+
+                    c_buf[m] = (q_buf[m] + r_buf[m]).astype(c_buf.dtype)
+                    store_c(q, m).start()
 
         @pl.when(s == SLOTS - 1)
         def _():
             for copy in load_b(0, 1):
                 copy.start()
 
-    for m in range(TILES):
-        store_c(n_blocks - 1, m).wait()
-        for h in range(2):
-            send_a(m, h).wait_send()
-
-    @pl.loop(n_blocks - SLOTS, n_blocks)
-    def _(s):
-        for m in range(TILES):
-            send_p(s, m).wait_send()
-
     @pl.loop(0, n_blocks)
     def _(t):
         for way in range(3):
             send_b(way, t).wait_send()
 
+    for m in range(TILES):
+        store_c(last - 2, m).wait()
+        store_q(last, m).wait()
+        for copy in store_p(m):
+            copy.wait()
+        for h in range(2):
+            send_a(m, h).wait_send()
+
+    @pl.loop(n_blocks - SLOTS, last)
+    def _(s):
+        for m in range(TILES):
+            send_p(s, m).wait_send()
+
+    for m in range(TILES):
+        send_p(last - 1, m).wait_recv()
+
+
+def write_out(n_done, c_ref, q_ref, r_ref, out_ref):
+    @pl.when(pl.program_id(0) < n_done)
+    def _():
+        out_ref[...] = c_ref[...]
+
+    @pl.when(pl.program_id(0) == n_done)
+    def _():
+        out_ref[...] = (q_ref[0] + r_ref[0]).astype(out_ref.dtype)
+
 
 def device_product(block, a_rows, b_rows):
     rows, _ = a_rows.shape
     depth, n_cols = b_rows.shape
-    n_blocks, tile = n_cols // block, rows // TILES
+    n_blocks, tile, early = n_cols // block, rows // TILES, block - LATE
+    last = n_blocks - 1
     anywhere = pl.BlockSpec(memory_space=pl.ANY)
     dma = pltpu.SemaphoreType.DMA
-    c_rows, _, _ = pl.pallas_call(
+    c_main, r_got, p_early, p_late, q_last, _ = pl.pallas_call(
         functools.partial(kernel, n_blocks, tile),
         out_shape=(
             jax.ShapeDtypeStruct((rows, n_cols), jnp.bfloat16),
+            jax.ShapeDtypeStruct((last, rows, block), jnp.float32),
+            jax.ShapeDtypeStruct((rows, early), jnp.float32),
+            jax.ShapeDtypeStruct((rows, LATE), jnp.float32),
+            jax.ShapeDtypeStruct((2, rows, block), jnp.float32),
             jax.ShapeDtypeStruct((3, n_blocks, depth, block), jnp.bfloat16),
-            jax.ShapeDtypeStruct((n_blocks, rows, block), jnp.float32),
         ),
         in_specs=[anywhere] * 2,
-        out_specs=(anywhere,) * 3,
+        out_specs=(anywhere,) * 6,
         scratch_shapes=[
             pltpu.VMEM((2, rows, 4 * depth), jnp.bfloat16),
             pltpu.VMEM((2, 4 * depth, block), jnp.bfloat16),
@@ -219,17 +271,39 @@
             dma((3, n_blocks)),
             dma((3, n_blocks)),
             dma((2, 4)),
-            dma((n_blocks, TILES)),
-            dma((n_blocks, TILES)),
+            dma((last, TILES)),
+            dma((last, TILES)),
             dma((TILES,)),
             dma((TILES,)),
+            dma((TILES,)),
+            dma((2, TILES)),
         ],
         compiler_params=pltpu.CompilerParams(
             collective_id=0, has_side_effects=True, vmem_limit_bytes=66_000_000
         ),
         name="split_sum_product",
     )(a_rows, b_rows)
-    return c_rows
+
+    swap = [(0, 1), (1, 0)]
+    got_early = lax.ppermute(p_early, "row", swap)
+    got_late = lax.ppermute(p_late, "row", swap)
+    out = pl.pallas_call(
+        functools.partial(write_out, last - 1),
+        grid=(last,),
+        out_shape=jax.ShapeDtypeStruct((rows, n_cols), jnp.bfloat16),
+        in_specs=[
+            pl.BlockSpec((rows, block), lambda i: (0, jnp.minimum(i, last - 2))),
+            pl.BlockSpec((1, rows, block), lambda i: (0, 0, 0)),
+            pl.BlockSpec((1, rows, block), lambda i: (last - 1, 0, 0)),
+        ],
+        out_specs=pl.BlockSpec((rows, block), lambda i: (0, i)),
+        cost_estimate=pl.CostEstimate(flops=20_000_000_000, bytes_accessed=4 * rows * n_cols, transcendentals=0),
+        name="write_out",
+    )(c_main, q_last, r_got)
+    for start, part in ((0, got_early), (early, got_late)):
+        own = lax.slice(q_last, (1, 0, start), (2, rows, start + part.shape[1]))[0]
+        out = lax.dynamic_update_slice(out, (own + part).astype(out.dtype), (0, last * block + start))
+    return out
 
 
 def solution(mesh, block=BLOCK):

time: 1290 us -> 1280 us (level)
  Pallas kernels: 1270 us -> 1240 us
  waiting for transfers between devices: 0 us -> 23 us
  local copies, waits for them, and re-layouts: 17.6 us -> 0 us
    pallas_call x1, Pallas kernels: 1270 us -> 1220 us  [device_product(): pl.pallas_call(functools.partial(kernel, n_blocks, tile), out_shape=(jax....]
    ppermute x0 -> x2, waiting for transfers between devices: none -> 23 us  [the longest x1 23 us: device_product(): got_early = lax.ppermute(p_early, 'row', swap)]
    pallas_call x0 -> x1, Pallas kernels: none -> 21.7 us  [device_product(): pl.pallas_call(functools.partial(write_out, last - 1), grid=(last,), out_...]
    unnamed x1 -> x0, local copies, waits for them, and re-layouts: 17.6 us -> none
  transfers between devices with their start and end apart: 0 -> 2, of which waited for: 0 -> 1; matrix products, arithmetic and copies ran while one was open for 0% -> 0% of each run, Pallas kernels for 0% -> 2%
where the time goes in v2:
time: 1280 us; the launch traced here: 1270 us
  Pallas kernels  1240 us (97%)
  waiting for transfers between devices  23 us (2%)
    pallas_call x1, Pallas kernels, device_product(): pl.pallas_call(functools.partial(kernel, n_blocks, tile), out_shape=(jax....  1220 us
  transfers between devices with their start and end apart: 2, of which 1 were waited for; matrix products, arithmetic and copies ran while one was open for 0% of the time, Pallas kernels for 2%

profile of v2, /device:TPU:0, one launch (start us, length us, event | category | flops | bytes accessed | tf_op | source)
XLA Modules:
  0.0 1272.8 jit_solution(9213773000063787191)
XLA Ops:
  0.0 1221.8 %split_sum_product.1 = (bf16[1024,10240]{1,0:T(8,128)(2,1)}, f32[19,1024,512]{2,1,0:T(8,128)}, f32[1024,384]{1,0:T(8,128)}, f32[1024,128]{1,0:T(8,128)}, f32[2,1...) custom-call(bf16[1024,16384]{1,0:T(8,128)(2,1)} %a_ref.1, bf16[2048,10240]{1,0:T(8,128)(2,1)} %b_ref.1), custom_call_target="tpu_custom_call" | custom-call | tf_op jit(solution)/shard_map/split_sum_product/pallas_call | solution.py:249
  1221.8 0.6 collective-permute-start.1
  1222.4 1.5 collective-permute-start
  1223.9 21.7 %write_out.1 = bf16[1024,10240]{1,0:T(8,128)(2,1)} custom-call(bf16[1024,10240]{1,0:T(8,128)(2,1)} %get-tuple-element.10.c_ref, f32[2,1024,512]{2,1,0:T(8,128)} %get-tuple-element.11.q_ref, f32[19,1024,512]{2,1,0:T(8,128)} %get-tuple-element.12.r_ref), custom_call_target="tpu_custom_call" | custom-call | flops 20000000000 | bytes 41943040 | tf_op jit(solution)/shard_map/write_out/pallas_call | solution.py:290
  1245.6 23.0 %collective-permute-done = f32[1024,384]{1,0:T(8,128)S(1)} collective-permute-done((f32[1024,384]{1,0:T(8,128)}, f32[1024,384]{1,0:T(8,128)S(1)}, u32[]{:S(2)}, u32[]{:S(2)}) %collective-permute-start) | collective-permute-done | bytes 1572896 | tf_op jit(solution)/shard_map/ppermute | solution.py:288
  1268.6 2.4 fusion.1
  1271.0 0.0 collective-permute-done.1
  1271.0 1.8 fusion.3
Async XLA Ops:
  1221.8 49.2 %collective-permute-start.1 = (f32[1024,128]{1,0:T(8,128)}, f32[1024,128]{1,0:T(8,128)S(1)}, u32[]{:S(2)}, u32[]{:S(2)}) collective-permute-start(f32[1024,128]{1,0:T(8,128)} %get-tuple-element.14), channel_id=1, source_target_pairs={{0,2},{2,0},{1,3},{3,1},{4,6},{6,4},{5,7},{7,5}} | collective-permute-start | bytes 1572872 | tf_op jit(solution)/shard_map/ppermute | solution.py:289
  1222.4 46.2 %collective-permute-start = (f32[1024,384]{1,0:T(8,128)}, f32[1024,384]{1,0:T(8,128)S(1)}, u32[]{:S(2)}, u32[]{:S(2)}) collective-permute-start(f32[1024,384]{1,0:T(8,128)} %get-tuple-element.13), channel_id=1, source_target_pairs={{0,2},{2,0},{1,3},{3,1},{4,6},{6,4},{5,7},{7,5}} | collective-permute-start | bytes 4718600 | tf_op jit(solution)/shard_map/ppermute | solution.py:288

commit v3 on v2

--- a/solution.py
+++ b/solution.py
@@ -14,12 +14,13 @@
 AHEAD = 4
 SLOTS = 3
 LATE = 128
+RING = 2 * (SLOTS + 1)
 
 
 def kernel(
     n_blocks, tile, a_ref, b_ref, c_ref, r_got, p_early, p_late, q_last, b_got,
     a_buf, b_buf, p_buf, q_buf, r_buf, c_buf,
-    a_own_sem, a_send, a_recv, b_send, b_recv, b_load_sem, p_send, r_recv, r_load_sem, c_sem, q_sem, last_sem,
+    a_own_sem, a_send, a_recv, b_send, b_recv, b_load_sem, first_send, first_recv, p_send, r_recv, r_load_sem, c_sem, q_sem, last_sem,
 ):
     last = n_blocks - 1
     col, row, core = lax.axis_index("col"), lax.axis_index("row"), lax.axis_index("depth")
@@ -49,7 +50,7 @@
     def send_b(way, t):
         return pltpu.make_async_remote_copy(
             src_ref=b_got.at[0, t] if way == 2 else b_ref.at[:, cols_of(t)], dst_ref=b_got.at[way, t],
-            send_sem=b_send.at[way, t], recv_sem=b_recv.at[way, t],
+            send_sem=b_send.at[way, lax.rem(t, RING)], recv_sem=b_recv.at[way, lax.rem(t, RING)],
             device_id=neighbour if way == 0 else sibling, device_id_type=MESH)
 
     def load_b(t, slot):
@@ -61,10 +62,15 @@
             for i, place in enumerate(places)
         ]
 
-    def send_p(s, m):
+    def send_first(m):
         return pltpu.make_async_remote_copy(
-            src_ref=p_buf.at[lax.rem(s, SLOTS), rows_of(m)], dst_ref=r_got.at[s, rows_of(m)],
-            send_sem=p_send.at[s, m], recv_sem=r_recv.at[s, m], device_id=partner, device_id_type=MESH)
+            src_ref=p_buf.at[0, rows_of(m)], dst_ref=r_got.at[0, rows_of(m)],
+            send_sem=first_send.at[m], recv_sem=first_recv.at[m], device_id=partner, device_id_type=MESH)
+
+    def send_block(s):
+        return pltpu.make_async_remote_copy(
+            src_ref=p_buf.at[lax.rem(s, SLOTS)], dst_ref=r_got.at[s],
+            send_sem=p_send.at[lax.rem(s, SLOTS)], recv_sem=r_recv.at[lax.rem(s, RING)], device_id=partner, device_id_type=MESH)
 
     def load_r(q, m):
         return pltpu.make_async_copy(r_got.at[q, rows_of(m)], r_buf.at[m], r_load_sem.at[m])
@@ -87,6 +93,15 @@
         return jnp.dot(a_buf[whose, rows_of(m), :], b_buf[slot], preferred_element_type=jnp.float32)
 
     def pass_on(t):
+        @pl.when(t >= RING - AHEAD)
+        def _():
+            send_b(0, t + AHEAD - RING).wait_send()
+
+        @pl.when(t >= RING)
+        def _():
+            send_b(1, t - RING).wait_send()
+            send_b(2, t - RING).wait_send()
+
         send_b(0, t).wait_recv()
         send_b(2, t).start()
         send_b(1, t).start()
@@ -134,6 +149,15 @@
                 for copy in load_b(s, 0):
                     copy.wait()
 
+            @pl.when(s == SLOTS)
+            def _():
+                for m in range(TILES):
+                    send_first(m).wait_send()
+
+            @pl.when(s > SLOTS)
+            def _():
+                send_block(s - SLOTS).wait_send()
+
             @pl.loop(0, TILES)
             def _(m):
                 @pl.when(s == 0)
@@ -141,21 +165,21 @@
                     for h in range(2):
                         send_a(m, h).wait_recv()
 
-                @pl.when(s >= SLOTS)
-                def _():
-                    send_p(s - SLOTS, m).wait_send()
-
                 p_buf[lax.rem(s, SLOTS), rows_of(m), :] = product(1, m, 0)
 
-                @pl.when(s < last)
-                def _():
-                    send_p(s, m).start()
+                @pl.when(s == 0)
+                def _():
+                    send_first(m).start()
 
                 @pl.when(s == last)
                 def _():
                     for copy in store_p(m):
                         copy.start()
 
+            @pl.when(jnp.logical_and(s > 0, s < last))
+            def _():
+                send_block(s).start()
+
             @pl.when(s + AHEAD < n_blocks)
             def _():
                 pass_on(s + AHEAD)
@@ -167,6 +191,21 @@
         @pl.when(s >= SLOTS)
         def _():
             q = s - SLOTS
+
+            @pl.when(q == 0)
+            def _():
+                for m in range(TILES):
+                    send_first(m).wait_recv()
+
+            @pl.when(jnp.logical_and(q > 0, q < last - 1))
+            def _():
+                send_block(q).wait_recv()
+
+            @pl.when(q < last - 1)
+            def _():
+                for m in range(TILES):
+                    load_r(q, m).start()
+
             for copy in load_b(q, 1):
                 copy.wait()
 
@@ -191,8 +230,6 @@
             def _():
                 @pl.loop(0, TILES)
                 def _(m):
-                    send_p(q, m).wait_recv()
-                    load_r(q, m).start()
                     load_r(q, m).wait()
 
                     @pl.when(q > 0)
@@ -207,10 +244,14 @@
             for copy in load_b(0, 1):
                 copy.start()
 
-    @pl.loop(0, n_blocks)
+    @pl.loop(n_blocks - RING, n_blocks)
     def _(t):
-        for way in range(3):
-            send_b(way, t).wait_send()
+        send_b(1, t).wait_send()
+        send_b(2, t).wait_send()
+
+        @pl.when(t >= n_blocks - RING + AHEAD)
+        def _():
+            send_b(0, t).wait_send()
 
     for m in range(TILES):
         store_c(last - 2, m).wait()
@@ -222,11 +263,9 @@
 
     @pl.loop(n_blocks - SLOTS, last)
     def _(s):
-        for m in range(TILES):
-            send_p(s, m).wait_send()
-
-    for m in range(TILES):
-        send_p(last - 1, m).wait_recv()
+        send_block(s).wait_send()
+
+    send_block(last - 1).wait_recv()
 
 
 def write_out(n_done, c_ref, q_ref, r_ref, out_ref):
@@ -268,11 +307,13 @@
             dma((2,)),
             dma((TILES, 2)),
             dma((TILES, 2)),
-            dma((3, n_blocks)),
-            dma((3, n_blocks)),
+            dma((3, RING)),
+            dma((3, RING)),
             dma((2, 4)),
-            dma((last, TILES)),
-            dma((last, TILES)),
+            dma((TILES,)),
+            dma((TILES,)),
+            dma((SLOTS,)),
+            dma((RING,)),
             dma((TILES,)),
             dma((TILES,)),
             dma((TILES,)),

time: 1280 us -> 1270 us (level)
  no operation moved by 1% of the time
where the time goes in v3:
time: 1270 us
  Pallas kernels  1240 us (98%)
  waiting for transfers between devices  23 us (2%)
    pallas_call x1, Pallas kernels, device_product(): pl.pallas_call(functools.partial(kernel, n_blocks, tile), out_shape=(jax....  1220 us
  transfers between devices with their start and end apart: 2, of which 1 were waited for; matrix products, arithmetic and copies ran while one was open for 0% of the time, Pallas kernels for 2%

profile of v3, /device:TPU:0, one launch (start us, length us, event | category | flops | bytes accessed | tf_op | source)
XLA Modules:
  0.0 1271.0 jit_solution(8595615336227154304)
XLA Ops:
  0.0 1220.0 %split_sum_product.1 = (bf16[1024,10240]{1,0:T(8,128)(2,1)}, f32[19,1024,512]{2,1,0:T(8,128)}, f32[1024,384]{1,0:T(8,128)}, f32[1024,128]{1,0:T(8,128)}, f32[2,1...) custom-call(bf16[1024,16384]{1,0:T(8,128)(2,1)} %a_ref.1, bf16[2048,10240]{1,0:T(8,128)(2,1)} %b_ref.1), custom_call_target="tpu_custom_call" | custom-call | tf_op jit(solution)/shard_map/split_sum_product/pallas_call | solution.py:288
  1220.0 0.6 collective-permute-start.1
  1220.5 1.5 collective-permute-start
  1222.0 21.7 %write_out.1 = bf16[1024,10240]{1,0:T(8,128)(2,1)} custom-call(bf16[1024,10240]{1,0:T(8,128)(2,1)} %get-tuple-element.10.c_ref, f32[2,1024,512]{2,1,0:T(8,128)} %get-tuple-element.11.q_ref, f32[19,1024,512]{2,1,0:T(8,128)} %get-tuple-element.12.r_ref), custom_call_target="tpu_custom_call" | custom-call | flops 20000000000 | bytes 41943040 | tf_op jit(solution)/shard_map/write_out/pallas_call | solution.py:331
  1243.8 23.0 %collective-permute-done = f32[1024,384]{1,0:T(8,128)S(1)} collective-permute-done((f32[1024,384]{1,0:T(8,128)}, f32[1024,384]{1,0:T(8,128)S(1)}, u32[]{:S(2)}, u32[]{:S(2)}) %collective-permute-start) | collective-permute-done | bytes 1572896 | tf_op jit(solution)/shard_map/ppermute | solution.py:329
  1266.7 2.4 fusion.1
  1269.2 0.0 collective-permute-done.1
  1269.2 1.8 fusion.3
Async XLA Ops:
  1220.0 49.2 %collective-permute-start.1 = (f32[1024,128]{1,0:T(8,128)}, f32[1024,128]{1,0:T(8,128)S(1)}, u32[]{:S(2)}, u32[]{:S(2)}) collective-permute-start(f32[1024,128]{1,0:T(8,128)} %get-tuple-element.14), channel_id=1, source_target_pairs={{0,2},{2,0},{1,3},{3,1},{4,6},{6,4},{5,7},{7,5}} | collective-permute-start | bytes 1572872 | tf_op jit(solution)/shard_map/ppermute | solution.py:330
  1220.5 46.2 %collective-permute-start = (f32[1024,384]{1,0:T(8,128)}, f32[1024,384]{1,0:T(8,128)S(1)}, u32[]{:S(2)}, u32[]{:S(2)}) collective-permute-start(f32[1024,384]{1,0:T(8,128)} %get-tuple-element.13), channel_id=1, source_target_pairs={{0,2},{2,0},{1,3},{3,1},{4,6},{6,4},{5,7},{7,5}} | collective-permute-start | bytes 4718600 | tf_op jit(solution)/shard_map/ppermute | solution.py:329

commit v4 on v3

--- a/solution.py
+++ b/solution.py
@@ -13,12 +13,12 @@
 TILES = 4
 AHEAD = 4
 SLOTS = 3
-LATE = 128
+LATE = 256
 RING = 2 * (SLOTS + 1)
 
 
 def kernel(
-    n_blocks, tile, a_ref, b_ref, c_ref, r_got, p_early, p_late, q_last, b_got,
+    n_blocks, tile, a_ref, b_ref, c_ref, r_got, p_early, p_late, q_early, q_late, q_done, b_got,
     a_buf, b_buf, p_buf, q_buf, r_buf, c_buf,
     a_own_sem, a_send, a_recv, b_send, b_recv, b_load_sem, first_send, first_recv, p_send, r_recv, r_load_sem, c_sem, q_sem, last_sem,
 ):
@@ -72,21 +72,27 @@
             src_ref=p_buf.at[lax.rem(s, SLOTS)], dst_ref=r_got.at[s],
             send_sem=p_send.at[lax.rem(s, SLOTS)], recv_sem=r_recv.at[lax.rem(s, RING)], device_id=partner, device_id_type=MESH)
 
-    def load_r(q, m):
-        return pltpu.make_async_copy(r_got.at[q, rows_of(m)], r_buf.at[m], r_load_sem.at[m])
-
-    def store_c(q, m):
-        return pltpu.make_async_copy(c_buf.at[m], c_ref.at[rows_of(m), cols_of(q)], c_sem.at[m])
-
-    def store_q(q, m):
-        return pltpu.make_async_copy(q_buf.at[m], q_last.at[q - last + 1, rows_of(m)], q_sem.at[m])
-
-    def store_p(m):
-        early = p_early.shape[1]
+    def load_r(q):
+        return pltpu.make_async_copy(r_got.at[q], r_buf, r_load_sem)
+
+    def store_c(q):
+        return pltpu.make_async_copy(c_buf, c_ref.at[:, cols_of(q)], c_sem)
+
+    parts = (pl.ds(0, p_early.shape[1]), pl.ds(p_early.shape[1], p_late.shape[1]))
+
+    def store_q_done():
+        return pltpu.make_async_copy(q_buf, q_done, q_sem.at[0])
+
+    def store_q():
         return [
-            pltpu.make_async_copy(
-                p_buf.at[last % SLOTS, rows_of(m), pl.ds(start, out.shape[1])], out.at[rows_of(m)], last_sem.at[i, m])
-            for i, (start, out) in enumerate(((0, p_early), (early, p_late)))
+            pltpu.make_async_copy(q_buf.at[:, part], out, q_sem.at[i])
+            for i, (part, out) in enumerate(zip(parts, (q_early, q_late)))
+        ]
+
+    def store_p():
+        return [
+            pltpu.make_async_copy(p_buf.at[last % SLOTS, :, part], out, last_sem.at[i])
+            for i, (part, out) in enumerate(zip(parts, (p_early, p_late)))
         ]
 
     def product(whose, m, slot):
@@ -171,10 +177,10 @@
                 def _():
                     send_first(m).start()
 
-                @pl.when(s == last)
-                def _():
-                    for copy in store_p(m):
-                        copy.start()
+            @pl.when(s == last)
+            def _():
+                for copy in store_p():
+                    copy.start()
 
             @pl.when(jnp.logical_and(s > 0, s < last))
             def _():
@@ -203,23 +209,27 @@
 
             @pl.when(q < last - 1)
             def _():
-                for m in range(TILES):
-                    load_r(q, m).start()
+                load_r(q).start()
 
             for copy in load_b(q, 1):
                 copy.wait()
 
+            @pl.when(q == last)
+            def _():
+                store_q_done().wait()
+
             @pl.loop(0, TILES)
             def _(m):
-                @pl.when(q == last)
-                def _():
-                    store_q(q - 1, m).wait()
-
-                q_buf[m] = product(0, m, 1)
-
-                @pl.when(q >= last - 1)
-                def _():
-                    store_q(q, m).start()
+                q_buf[rows_of(m), :] = product(0, m, 1)
+
+            @pl.when(q == last - 1)
+            def _():
+                store_q_done().start()
+
+            @pl.when(q == last)
+            def _():
+                for copy in store_q():
+                    copy.start()
 
             @pl.when(q + 1 < n_blocks)
             def _():
@@ -228,16 +238,18 @@
 
             @pl.when(q < last - 1)
             def _():
+                load_r(q).wait()
+
+                @pl.when(q > 0)
+                def _():
+                    store_c(q - 1).wait()
+
                 @pl.loop(0, TILES)
                 def _(m):
-                    load_r(q, m).wait()
-
-                    @pl.when(q > 0)
-                    def _():
-                        store_c(q - 1, m).wait()
-
-                    c_buf[m] = (q_buf[m] + r_buf[m]).astype(c_buf.dtype)
-                    store_c(q, m).start()
+                    rows = rows_of(m)
+                    c_buf[rows, :] = (q_buf[rows, :] + r_buf[rows, :]).astype(c_buf.dtype)
+
+                store_c(q).start()
 
         @pl.when(s == SLOTS - 1)
         def _():
@@ -253,11 +265,10 @@
         def _():
             send_b(0, t).wait_send()
 
+    store_c(last - 2).wait()
+    for copy in store_q() + store_p():
+        copy.wait()
     for m in range(TILES):
-        store_c(last - 2, m).wait()
-        store_q(last, m).wait()
-        for copy in store_p(m):
-            copy.wait()
         for h in range(2):
             send_a(m, h).wait_send()
 
@@ -275,7 +286,7 @@
 
     @pl.when(pl.program_id(0) == n_done)
     def _():
-        out_ref[...] = (q_ref[0] + r_ref[0]).astype(out_ref.dtype)
+        out_ref[...] = (q_ref[...] + r_ref[0]).astype(out_ref.dtype)
 
 
 def device_product(block, a_rows, b_rows):
@@ -285,25 +296,27 @@
     last = n_blocks - 1
     anywhere = pl.BlockSpec(memory_space=pl.ANY)
     dma = pltpu.SemaphoreType.DMA
-    c_main, r_got, p_early, p_late, q_last, _ = pl.pallas_call(
+    c_main, r_got, p_early, p_late, q_early, q_late, q_done, _ = pl.pallas_call(
         functools.partial(kernel, n_blocks, tile),
         out_shape=(
             jax.ShapeDtypeStruct((rows, n_cols), jnp.bfloat16),
             jax.ShapeDtypeStruct((last, rows, block), jnp.float32),
             jax.ShapeDtypeStruct((rows, early), jnp.float32),
             jax.ShapeDtypeStruct((rows, LATE), jnp.float32),
-            jax.ShapeDtypeStruct((2, rows, block), jnp.float32),
+            jax.ShapeDtypeStruct((rows, early), jnp.float32),
+            jax.ShapeDtypeStruct((rows, LATE), jnp.float32),
+            jax.ShapeDtypeStruct((rows, block), jnp.float32),
             jax.ShapeDtypeStruct((3, n_blocks, depth, block), jnp.bfloat16),
         ),
         in_specs=[anywhere] * 2,
-        out_specs=(anywhere,) * 6,
+        out_specs=(anywhere,) * 8,
         scratch_shapes=[
             pltpu.VMEM((2, rows, 4 * depth), jnp.bfloat16),
             pltpu.VMEM((2, 4 * depth, block), jnp.bfloat16),
             pltpu.VMEM((SLOTS, rows, block), jnp.float32),
-            pltpu.VMEM((TILES, tile, block), jnp.float32),
-            pltpu.VMEM((TILES, tile, block), jnp.float32),
-            pltpu.VMEM((TILES, tile, block), jnp.bfloat16),
+            pltpu.VMEM((rows, block), jnp.float32),
+            pltpu.VMEM((rows, block), jnp.float32),
+            pltpu.VMEM((rows, block), jnp.bfloat16),
             dma((2,)),
             dma((TILES, 2)),
             dma((TILES, 2)),
@@ -314,10 +327,10 @@
             dma((TILES,)),
             dma((SLOTS,)),
             dma((RING,)),
-            dma((TILES,)),
-            dma((TILES,)),
-            dma((TILES,)),
-            dma((2, TILES)),
+            dma,
+            dma,
+            dma((2,)),
+            dma((2,)),
         ],
         compiler_params=pltpu.CompilerParams(
             collective_id=0, has_side_effects=True, vmem_limit_bytes=66_000_000
@@ -334,15 +347,14 @@
         out_shape=jax.ShapeDtypeStruct((rows, n_cols), jnp.bfloat16),
         in_specs=[
             pl.BlockSpec((rows, block), lambda i: (0, jnp.minimum(i, last - 2))),
-            pl.BlockSpec((1, rows, block), lambda i: (0, 0, 0)),
+            pl.BlockSpec((rows, block), lambda i: (0, 0)),
             pl.BlockSpec((1, rows, block), lambda i: (last - 1, 0, 0)),
         ],
         out_specs=pl.BlockSpec((rows, block), lambda i: (0, i)),
         cost_estimate=pl.CostEstimate(flops=20_000_000_000, bytes_accessed=4 * rows * n_cols, transcendentals=0),
         name="write_out",
-    )(c_main, q_last, r_got)
-    for start, part in ((0, got_early), (early, got_late)):
-        own = lax.slice(q_last, (1, 0, start), (2, rows, start + part.shape[1]))[0]
+    )(c_main, q_done, r_got)
+    for start, own, part in ((0, q_early, got_early), (early, q_late, got_late)):
         out = lax.dynamic_update_slice(out, (own + part).astype(out.dtype), (0, last * block + start))
     return out
 

time: 1270 us -> 1270 us (level)
    ppermute x1, waiting for transfers between devices: 23 us -> 2.45 us  [device_product(): got_early = lax.ppermute(p_early, 'row', swap)]
    ppermute x1, waiting for transfers between devices: 0.01 us -> 18.3 us  [device_product(): got_late = lax.ppermute(p_late, 'row', swap)]
  transfers between devices with their start and end apart: 2 -> 2, of which waited for: 1 -> 2; matrix products, arithmetic and copies ran while one was open for 0% -> 0% of each run, Pallas kernels for 2% -> 2%
where the time goes in v4:
time: 1270 us
  Pallas kernels  1240 us (98%)
  waiting for transfers between devices  20.7 us (2%)
    pallas_call x1, Pallas kernels, device_product(): pl.pallas_call(functools.partial(kernel, n_blocks, tile), out_shape=(jax....  1220 us
  transfers between devices with their start and end apart: 2, of which 2 were waited for; matrix products, arithmetic and copies ran while one was open for 0% of the time, Pallas kernels for 2%

profile of v4, /device:TPU:0, one launch (start us, length us, event | category | flops | bytes accessed | tf_op | source)
XLA Modules:
  0.0 1267.5 jit_solution(6359893629784227049)
XLA Ops:
  0.0 1219.9 %split_sum_product.1 = (bf16[1024,10240]{1,0:T(8,128)(2,1)}, f32[19,1024,512]{2,1,0:T(8,128)}, f32[1024,256]{1,0:T(8,128)}, f32[1024,256]{1,0:T(8,128)}, f32[102...) custom-call(bf16[1024,16384]{1,0:T(8,128)(2,1)} %a_ref.1, ...), custom_call_target="tpu_custom_call" | custom-call | tf_op jit(solution)/shard_map/split_sum_product/pallas_call | solution.py:299
  1219.9 0.6 collective-permute-start
  1220.4 1.5 collective-permute-start.1
  1221.9 0.0 copy-start.1
  1221.9 0.0 copy-start
  1221.9 21.9 %write_out.1 = bf16[1024,10240]{1,0:T(8,128)(2,1)} custom-call(bf16[1024,10240]{1,0:T(8,128)(2,1)} %get-tuple-element.12.c_ref, f32[1024,512]{1,0:T(8,128)} %get-tuple-element.13.q_ref, f32[19,1024,512]{2,1,0:T(8,128)} %get-tuple-element.14.r_ref), custom_call_target="tpu_custom_call" | custom-call | flops 20000000000 | bytes 41943040 | tf_op jit(solution)/shard_map/write_out/pallas_call | solution.py:344
  1243.8 2.5 collective-permute-done
  1246.2 0.0 copy-done.1
  1246.2 2.1 fusion
  1248.3 18.3 %collective-permute-done.1 = f32[1024,256]{1,0:T(8,128)S(1)} collective-permute-done((f32[1024,256]{1,0:T(8,128)}, f32[1024,256]{1,0:T(8,128)S(1)}, u32[]{:S(2)}, u32[]{:S(2)}) %collective-permute-start.1) | collective-permute-done | bytes 1048608 | tf_op jit(solution)/shard_map/ppermute | solution.py:343
  1266.6 0.0 copy-done
  1266.6 0.9 fusion.1
Async XLA Ops:
  1219.9 26.4 %collective-permute-start = (f32[1024,256]{1,0:T(8,128)}, f32[1024,256]{1,0:T(8,128)}, u32[]{:S(2)}, u32[]{:S(2)}) collective-permute-start(f32[1024,256]{1,0:T(8,128)} %get-tuple-element.16), channel_id=1, source_target_pairs={{0,2},{2,0},{1,3},{3,1},{4,6},{6,4},{5,7},{7,5}} | collective-permute-start | bytes 3145736 | tf_op jit(solution)/shard_map/ppermute | solution.py:342
  1220.4 46.2 %collective-permute-start.1 = (f32[1024,256]{1,0:T(8,128)}, f32[1024,256]{1,0:T(8,128)S(1)}, u32[]{:S(2)}, u32[]{:S(2)}) collective-permute-start(f32[1024,256]{1,0:T(8,128)} %get-tuple-element.18), channel_id=1, source_target_pairs={{0,2},{2,0},{1,3},{3,1},{4,6},{6,4},{5,7},{7,5}} | collective-permute-start | bytes 3145736 | tf_op jit(solution)/shard_map/ppermute | solution.py:343
  1221.9 24.3 %copy-start.1 = (f32[1024,256]{1,0:T(8,128)S(1)}, f32[1024,256]{1,0:T(8,128)}, u32[]{:S(2)}) copy-start(f32[1024,256]{1,0:T(8,128)} %get-tuple-element.15) | copy-start | bytes 3145732
  1221.9 44.7 %copy-start = (f32[1024,256]{1,0:T(8,128)S(1)}, f32[1024,256]{1,0:T(8,128)}, u32[]{:S(2)}) copy-start(f32[1024,256]{1,0:T(8,128)} %get-tuple-element.17) | copy-start | bytes 3145732

commit v5 on v4

--- a/solution.py
+++ b/solution.py
@@ -127,22 +127,40 @@
         pl.semaphore_signal(barrier, inc=1, device_id=other, device_id_type=MESH)
     pl.semaphore_wait(barrier, 3)
 
-    for m in range(TILES):
-        for h in range(2):
-            send_a(m, h).start()
-        if m == 0:
-            for t in range(AHEAD):
-                send_b(0, t).start()
-    for h in range(2):
-        own_a(h).start()
+    def start_a(tiles):
+        for m in tiles:
+            for h in range(2):
+                send_a(m, h).start()
+
+    early, late = range(2), range(2, TILES)
+    start_a(early)
+    for t in range(AHEAD):
+        send_b(0, t).start()
+
+    @pl.when(core == 0)
+    def _():
+        start_a(late)
 
     @pl.loop(0, AHEAD)
     def _(t):
         pass_on(t)
 
-    start_load_first(0)
+    @pl.when(core == 1)
+    def _():
+        for m in early:
+            for h in range(2):
+                send_a(m, h).wait_send()
+
+    for h in range(2):
+        own_a(h).start()
     for h in range(2):
         own_a(h).wait()
+
+    @pl.when(core == 1)
+    def _():
+        start_a(late)
+
+    start_load_first(0)
     for copy in load_b(0, 0):
         copy.wait()
 
@@ -268,8 +286,13 @@
     store_c(last - 2).wait()
     for copy in store_q() + store_p():
         copy.wait()
-    for m in range(TILES):
-        for h in range(2):
+    for h in range(2):
+        @pl.when(core == 0)
+        def _():
+            for m in early:
+                send_a(m, h).wait_send()
+
+        for m in late:
             send_a(m, h).wait_send()
 
     @pl.loop(n_blocks - SLOTS, last)

time: 1270 us -> 1260 us (level)
  transfers between devices with their start and end apart: 2 -> 2, of which waited for: 2 -> 1; matrix products, arithmetic and copies ran while one was open for 0% -> 0% of each run, Pallas kernels for 2% -> 2%
where the time goes in v5:
time: 1260 us
  Pallas kernels  1230 us (98%)
  waiting for transfers between devices  18.8 us (1%)
    pallas_call x1, Pallas kernels, device_product(): pl.pallas_call(functools.partial(kernel, n_blocks, tile), out_shape=(jax....  1210 us
  transfers between devices with their start and end apart: 2, of which 1 were waited for; matrix products, arithmetic and copies ran while one was open for 0% of the time, Pallas kernels for 2%

profile of v5, /device:TPU:0, one launch (start us, length us, event | category | flops | bytes accessed | tf_op | source)
XLA Modules:
  0.0 1258.3 jit_solution(1238024246378308989)
XLA Ops:
  0.0 1212.6 %split_sum_product.1 = (bf16[1024,10240]{1,0:T(8,128)(2,1)}, f32[19,1024,512]{2,1,0:T(8,128)}, f32[1024,256]{1,0:T(8,128)}, f32[1024,256]{1,0:T(8,128)}, f32[102...) custom-call(bf16[1024,16384]{1,0:T(8,128)(2,1)} %a_ref.1, ...), custom_call_target="tpu_custom_call" | custom-call | tf_op jit(solution)/shard_map/split_sum_product/pallas_call | solution.py:322
  1212.6 0.4 collective-permute-start
  1213.0 1.6 collective-permute-start.1
  1214.6 0.0 copy-start.1
  1214.6 0.0 copy-start
  1214.6 21.9 %write_out.1 = bf16[1024,10240]{1,0:T(8,128)(2,1)} custom-call(bf16[1024,10240]{1,0:T(8,128)(2,1)} %get-tuple-element.12.c_ref, f32[1024,512]{1,0:T(8,128)} %get-tuple-element.13.q_ref, f32[19,1024,512]{2,1,0:T(8,128)} %get-tuple-element.14.r_ref), custom_call_target="tpu_custom_call" | custom-call | flops 20000000000 | bytes 41943040 | tf_op jit(solution)/shard_map/write_out/pallas_call | solution.py:367
  1236.5 0.0 collective-permute-done
  1236.5 0.0 copy-done.1
  1236.5 2.1 fusion
  1238.6 18.8 %collective-permute-done.1 = f32[1024,256]{1,0:T(8,128)S(1)} collective-permute-done((f32[1024,256]{1,0:T(8,128)}, f32[1024,256]{1,0:T(8,128)S(1)}, u32[]{:S(2)}, u32[]{:S(2)}) %collective-permute-start.1) | collective-permute-done | bytes 1048608 | tf_op jit(solution)/shard_map/ppermute | solution.py:366
  1257.4 0.0 copy-done
  1257.4 0.9 fusion.1
Async XLA Ops:
  1212.6 23.9 %collective-permute-start = (f32[1024,256]{1,0:T(8,128)}, f32[1024,256]{1,0:T(8,128)}, u32[]{:S(2)}, u32[]{:S(2)}) collective-permute-start(f32[1024,256]{1,0:T(8,128)} %get-tuple-element.16), channel_id=1, source_target_pairs={{0,2},{2,0},{1,3},{3,1},{4,6},{6,4},{5,7},{7,5}} | collective-permute-start | bytes 3145736 | tf_op jit(solution)/shard_map/ppermute | solution.py:365
  1213.0 44.4 %collective-permute-start.1 = (f32[1024,256]{1,0:T(8,128)}, f32[1024,256]{1,0:T(8,128)S(1)}, u32[]{:S(2)}, u32[]{:S(2)}) collective-permute-start(f32[1024,256]{1,0:T(8,128)} %get-tuple-element.18), channel_id=1, source_target_pairs={{0,2},{2,0},{1,3},{3,1},{4,6},{6,4},{5,7},{7,5}} | collective-permute-start | bytes 3145736 | tf_op jit(solution)/shard_map/ppermute | solution.py:366
  1214.6 21.9 %copy-start.1 = (f32[1024,256]{1,0:T(8,128)S(1)}, f32[1024,256]{1,0:T(8,128)}, u32[]{:S(2)}) copy-start(f32[1024,256]{1,0:T(8,128)} %get-tuple-element.15) | copy-start | bytes 3145732
  1214.6 42.8 %copy-start = (f32[1024,256]{1,0:T(8,128)S(1)}, f32[1024,256]{1,0:T(8,128)}, u32[]{:S(2)}) copy-start(f32[1024,256]{1,0:T(8,128)} %get-tuple-element.17) | copy-start | bytes 3145732

commit v6 on v5

--- a/solution.py
+++ b/solution.py
@@ -13,14 +13,15 @@
 TILES = 4
 AHEAD = 4
 SLOTS = 3
-LATE = 256
+LATE = 128
+PIECES = 2
 RING = 2 * (SLOTS + 1)
 
 
 def kernel(
     n_blocks, tile, a_ref, b_ref, c_ref, r_got, p_early, p_late, q_early, q_late, q_done, b_got,
     a_buf, b_buf, p_buf, q_buf, r_buf, c_buf,
-    a_own_sem, a_send, a_recv, b_send, b_recv, b_load_sem, first_send, first_recv, p_send, r_recv, r_load_sem, c_sem, q_sem, last_sem,
+    a_own_sem, a_send, a_recv, b_send, b_recv, b_load_sem, first_send, first_recv, p_send, r_recv, r_load_sem, c_sem, q_sem, last_sem, here_sem,
 ):
     last = n_blocks - 1
     col, row, core = lax.axis_index("col"), lax.axis_index("row"), lax.axis_index("depth")
@@ -78,20 +79,20 @@
     def store_c(q):
         return pltpu.make_async_copy(c_buf, c_ref.at[:, cols_of(q)], c_sem)
 
-    parts = (pl.ds(0, p_early.shape[1]), pl.ds(p_early.shape[1], p_late.shape[1]))
+    parts = (pl.ds(0, p_early.shape[0]), pl.ds(p_early.shape[0], p_late.shape[0]))
 
     def store_q_done():
         return pltpu.make_async_copy(q_buf, q_done, q_sem.at[0])
 
     def store_q():
         return [
-            pltpu.make_async_copy(q_buf.at[:, part], out, q_sem.at[i])
+            pltpu.make_async_copy(q_buf.at[part], out, q_sem.at[i])
             for i, (part, out) in enumerate(zip(parts, (q_early, q_late)))
         ]
 
     def store_p():
         return [
-            pltpu.make_async_copy(p_buf.at[last % SLOTS, :, part], out, last_sem.at[i])
+            pltpu.make_async_copy(p_buf.at[last % SLOTS, part], out, last_sem.at[i])
             for i, (part, out) in enumerate(zip(parts, (p_early, p_late)))
         ]
 
@@ -123,9 +124,32 @@
             copy.start()
 
     barrier = pltpu.get_barrier_semaphore()
-    for other in (neighbour, partner, sibling):
-        pl.semaphore_signal(barrier, inc=1, device_id=other, device_id_type=MESH)
-    pl.semaphore_wait(barrier, 3)
+    root = jnp.logical_and(col == 0, core == 0)
+    pl.semaphore_signal(barrier, inc=1, device_id=partner, device_id_type=MESH)
+
+    @pl.when(jnp.logical_or(root, col == 1))
+    def _():
+        pl.semaphore_signal(barrier, inc=1, device_id=sibling, device_id_type=MESH)
+
+    @pl.when(jnp.logical_or(root, core == 1))
+    def _():
+        pl.semaphore_signal(barrier, inc=1, device_id=neighbour, device_id_type=MESH)
+
+    @pl.when(root)
+    def _():
+        pl.semaphore_wait(barrier, 1)
+
+    @pl.when(jnp.logical_not(root))
+    def _():
+        pl.semaphore_wait(barrier, 3)
+
+    @pl.when(jnp.logical_and(col == 0, core == 1))
+    def _():
+        pl.semaphore_signal(here_sem, inc=1, device_id=sibling, device_id_type=MESH)
+
+    @pl.when(jnp.logical_and(col == 1, core == 0))
+    def _():
+        pl.semaphore_signal(here_sem, inc=1, device_id=neighbour, device_id_type=MESH)
 
     def start_a(tiles):
         for m in tiles:
@@ -134,6 +158,11 @@
 
     early, late = range(2), range(2, TILES)
     start_a(early)
+
+    @pl.when(root)
+    def _():
+        pl.semaphore_wait(here_sem, 2)
+
     for t in range(AHEAD):
         send_b(0, t).start()
 
@@ -141,7 +170,16 @@
     def _():
         start_a(late)
 
-    @pl.loop(0, AHEAD)
+    @pl.when(core == 0)
+    def _():
+        for h in range(2):
+            own_a(h).start()
+
+    pass_on(0)
+    pass_on(1)
+    start_load_first(0)
+
+    @pl.loop(2, AHEAD)
     def _(t):
         pass_on(t)
 
@@ -150,9 +188,9 @@
         for m in early:
             for h in range(2):
                 send_a(m, h).wait_send()
-
-    for h in range(2):
-        own_a(h).start()
+        for h in range(2):
+            own_a(h).start()
+
     for h in range(2):
         own_a(h).wait()
 
@@ -160,7 +198,6 @@
     def _():
         start_a(late)
 
-    start_load_first(0)
     for copy in load_b(0, 0):
         copy.wait()
 
@@ -302,20 +339,41 @@
     send_block(last - 1).wait_recv()
 
 
-def write_out(n_done, c_ref, q_ref, r_ref, out_ref):
-    @pl.when(pl.program_id(0) < n_done)
-    def _():
-        out_ref[...] = c_ref[...]
-
-    @pl.when(pl.program_id(0) == n_done)
-    def _():
-        out_ref[...] = (q_ref[...] + r_ref[0]).astype(out_ref.dtype)
+def write_out(c_ref, q_ref, r_ref, out_ref, c_buf, q_buf, r_buf, o_buf, load_sem, store_sem):
+    rows, done = c_buf.shape
+    step = rows // PIECES
+
+    def load(i):
+        some = pl.ds(i * step, step)
+        return pltpu.make_async_copy(c_ref.at[some, pl.ds(0, done)], c_buf.at[some], load_sem.at[i])
+
+    def store(i):
+        some = pl.ds(i * step, step)
+        return pltpu.make_async_copy(c_buf.at[some], out_ref.at[some, pl.ds(0, done)], store_sem.at[i])
+
+    load_q = pltpu.make_async_copy(q_ref, q_buf, load_sem.at[PIECES])
+    load_r = pltpu.make_async_copy(r_ref.at[r_ref.shape[0] - 1], r_buf, load_sem.at[PIECES + 1])
+    store_sum = pltpu.make_async_copy(o_buf, out_ref.at[:, pl.ds(done, o_buf.shape[1])], store_sem.at[PIECES])
+    for i in range(PIECES):
+        load(i).start()
+    load_q.start()
+    load_r.start()
+    for i in range(PIECES):
+        load(i).wait()
+        store(i).start()
+    load_q.wait()
+    load_r.wait()
+    o_buf[...] = (q_buf[...] + r_buf[...]).astype(o_buf.dtype)
+    store_sum.start()
+    for i in range(PIECES):
+        store(i).wait()
+    store_sum.wait()
 
 
 def device_product(block, a_rows, b_rows):
     rows, _ = a_rows.shape
     depth, n_cols = b_rows.shape
-    n_blocks, tile, early = n_cols // block, rows // TILES, block - LATE
+    n_blocks, tile, early = n_cols // block, rows // TILES, rows - LATE
     last = n_blocks - 1
     anywhere = pl.BlockSpec(memory_space=pl.ANY)
     dma = pltpu.SemaphoreType.DMA
@@ -324,10 +382,10 @@
         out_shape=(
             jax.ShapeDtypeStruct((rows, n_cols), jnp.bfloat16),
             jax.ShapeDtypeStruct((last, rows, block), jnp.float32),
-            jax.ShapeDtypeStruct((rows, early), jnp.float32),
-            jax.ShapeDtypeStruct((rows, LATE), jnp.float32),
-            jax.ShapeDtypeStruct((rows, early), jnp.float32),
-            jax.ShapeDtypeStruct((rows, LATE), jnp.float32),
+            jax.ShapeDtypeStruct((early, block), jnp.float32),
+            jax.ShapeDtypeStruct((LATE, block), jnp.float32),
+            jax.ShapeDtypeStruct((early, block), jnp.float32),
+            jax.ShapeDtypeStruct((LATE, block), jnp.float32),
             jax.ShapeDtypeStruct((rows, block), jnp.float32),
             jax.ShapeDtypeStruct((3, n_blocks, depth, block), jnp.bfloat16),
         ),
@@ -354,6 +412,7 @@
             dma,
             dma((2,)),
             dma((2,)),
+            pltpu.SemaphoreType.REGULAR,
         ],
         compiler_params=pltpu.CompilerParams(
             collective_id=0, has_side_effects=True, vmem_limit_bytes=66_000_000
@@ -365,20 +424,23 @@
     got_early = lax.ppermute(p_early, "row", swap)
     got_late = lax.ppermute(p_late, "row", swap)
     out = pl.pallas_call(
-        functools.partial(write_out, last - 1),
-        grid=(last,),
+        write_out,
         out_shape=jax.ShapeDtypeStruct((rows, n_cols), jnp.bfloat16),
-        in_specs=[
-            pl.BlockSpec((rows, block), lambda i: (0, jnp.minimum(i, last - 2))),
-            pl.BlockSpec((rows, block), lambda i: (0, 0)),
-            pl.BlockSpec((1, rows, block), lambda i: (last - 1, 0, 0)),
+        in_specs=[anywhere] * 3,
+        out_specs=anywhere,
+        scratch_shapes=[
+            pltpu.VMEM((rows, (last - 1) * block), jnp.bfloat16),
+            pltpu.VMEM((rows, block), jnp.float32),
+            pltpu.VMEM((rows, block), jnp.float32),
+            pltpu.VMEM((rows, block), jnp.bfloat16),
+            dma((PIECES + 2,)),
+            dma((PIECES + 1,)),
         ],
-        out_specs=pl.BlockSpec((rows, block), lambda i: (0, i)),
         cost_estimate=pl.CostEstimate(flops=20_000_000_000, bytes_accessed=4 * rows * n_cols, transcendentals=0),
         name="write_out",
     )(c_main, q_done, r_got)
     for start, own, part in ((0, q_early, got_early), (early, q_late, got_late)):
-        out = lax.dynamic_update_slice(out, (own + part).astype(out.dtype), (0, last * block + start))
+        out = lax.dynamic_update_slice(out, (own + part).astype(out.dtype), (start, last * block))
     return out
 
 

time: 1260 us -> 1270 us (level)
    ppermute x1, waiting for transfers between devices: 0.01 us -> 28.6 us  [device_product(): got_early = lax.ppermute(p_early, 'row', swap)]
    ppermute x1, waiting for transfers between devices: 18.8 us -> 0.01 us  [device_product(): got_late = lax.ppermute(p_late, 'row', swap)]
  transfers between devices with their start and end apart: 2 -> 2, of which waited for: 1 -> 1; matrix products, arithmetic and copies ran while one was open for 0% -> 0% of each run, Pallas kernels for 2% -> 1%
where the time goes in v6:
time: 1270 us; the launch traced here: 1260 us
  Pallas kernels  1230 us (97%)
  waiting for transfers between devices  28.6 us (2%)
    pallas_call x1, Pallas kernels, device_product(): pl.pallas_call(functools.partial(kernel, n_blocks, tile), out_shape=(jax....  1210 us
    ppermute x1, waiting for transfers between devices, device_product(): got_early = lax.ppermute(p_early, 'row', swap)  28.6 us
  transfers between devices with their start and end apart: 2, of which 1 were waited for; matrix products, arithmetic and copies ran while one was open for 0% of the time, Pallas kernels for 1%

profile of v6, /device:TPU:0, one launch (start us, length us, event | category | flops | bytes accessed | tf_op | source)
XLA Modules:
  0.0 1260.1 jit_solution(10482594953116030871)
XLA Ops:
  0.0 1211.8 %split_sum_product.1 = (bf16[1024,10240]{1,0:T(8,128)(2,1)}, f32[19,1024,512]{2,1,0:T(8,128)}, f32[896,512]{1,0:T(8,128)}, f32[128,512]{1,0:T(8,128)}, f32[896,5...) custom-call(bf16[1024,16384]{1,0:T(8,128)(2,1)} %a_ref.1, ...), custom_call_target="tpu_custom_call" | custom-call | tf_op jit(solution)/shard_map/split_sum_product/pallas_call | solution.py:380
  1211.8 1.2 collective-permute-start.1
  1213.0 0.8 collective-permute-start
  1213.9 0.0 copy-start
  1213.9 0.0 copy-start.1
  1213.9 14.2 %write_out.1 = bf16[1024,10240]{1,0:T(8,128)(2,1)} custom-call(bf16[1024,10240]{1,0:T(8,128)(2,1)} %get-tuple-element.12.c_ref, f32[1024,512]{1,0:T(8,128)} %get-tuple-element.13.q_ref, f32[19,1024,512]{2,1,0:T(8,128)} %get-tuple-element.14.r_ref), custom_call_target="tpu_custom_call" | custom-call | flops 20000000000 | bytes 41943040 | tf_op jit(solution)/shard_map/write_out/pallas_call | solution.py:426
  1228.1 28.6 %collective-permute-done = f32[896,512]{1,0:T(8,128)} collective-permute-done((f32[896,512]{1,0:T(8,128)}, f32[896,512]{1,0:T(8,128)}, u32[]{:S(2)}, u32[]{:S(2)}) %collective-permute-start) | collective-permute-done | bytes 1835040 | tf_op jit(solution)/shard_map/ppermute | solution.py:424
  1256.7 0.0 copy-done
  1256.7 2.7 fusion
  1259.4 0.0 collective-permute-done.1
  1259.4 0.0 copy-done.1
  1259.4 0.7 fusion.1
Async XLA Ops:
  1211.8 47.6 %collective-permute-start.1 = (f32[128,512]{1,0:T(8,128)}, f32[128,512]{1,0:T(8,128)S(1)}, u32[]{:S(2)}, u32[]{:S(2)}) collective-permute-start(f32[128,512]{1,0:T(8,128)} %get-tuple-element.18), channel_id=1, source_target_pairs={{0,2},{2,0},{1,3},{3,1},{4,6},{6,4},{5,7},{7,5}} | collective-permute-start | bytes 786440 | tf_op jit(solution)/shard_map/ppermute | solution.py:425
  1213.0 43.7 %collective-permute-start = (f32[896,512]{1,0:T(8,128)}, f32[896,512]{1,0:T(8,128)}, u32[]{:S(2)}, u32[]{:S(2)}) collective-permute-start(f32[896,512]{1,0:T(8,128)} %get-tuple-element.16), channel_id=1, source_target_pairs={{0,2},{2,0},{1,3},{3,1},{4,6},{6,4},{5,7},{7,5}} | collective-permute-start | bytes 5505032 | tf_op jit(solution)/shard_map/ppermute | solution.py:424
  1213.9 42.9 %copy-start = (f32[896,512]{1,0:T(8,128)S(1)}, f32[896,512]{1,0:T(8,128)}, u32[]{:S(2)}) copy-start(f32[896,512]{1,0:T(8,128)} %get-tuple-element.15) | copy-start | bytes 5505028
  1213.9 45.6 %copy-start.1 = (f32[128,512]{1,0:T(8,128)S(1)}, f32[128,512]{1,0:T(8,128)}, u32[]{:S(2)}) copy-start(f32[128,512]{1,0:T(8,128)} %get-tuple-element.17) | copy-start | bytes 786436

commit v7 on v6

--- a/solution.py
+++ b/solution.py
@@ -14,6 +14,7 @@
 AHEAD = 4
 SLOTS = 3
 LATE = 128
+HUB = (1, 0)
 PIECES = 2
 RING = 2 * (SLOTS + 1)
 
@@ -124,32 +125,20 @@
             copy.start()
 
     barrier = pltpu.get_barrier_semaphore()
-    root = jnp.logical_and(col == 0, core == 0)
+    is_hub = jnp.logical_and(col == HUB[0], core == HUB[1])
     pl.semaphore_signal(barrier, inc=1, device_id=partner, device_id_type=MESH)
 
-    @pl.when(jnp.logical_or(root, col == 1))
-    def _():
-        pl.semaphore_signal(barrier, inc=1, device_id=sibling, device_id_type=MESH)
-
-    @pl.when(jnp.logical_or(root, core == 1))
-    def _():
-        pl.semaphore_signal(barrier, inc=1, device_id=neighbour, device_id_type=MESH)
-
-    @pl.when(root)
-    def _():
+    @pl.when(jnp.logical_not(is_hub))
+    def _():
+        hub = {"col": HUB[0], "depth": HUB[1]}
+        pl.semaphore_signal(barrier, inc=1, device_id=hub, device_id_type=MESH)
         pl.semaphore_wait(barrier, 1)
 
-    @pl.when(jnp.logical_not(root))
-    def _():
-        pl.semaphore_wait(barrier, 3)
-
-    @pl.when(jnp.logical_and(col == 0, core == 1))
-    def _():
-        pl.semaphore_signal(here_sem, inc=1, device_id=sibling, device_id_type=MESH)
-
-    @pl.when(jnp.logical_and(col == 1, core == 0))
-    def _():
-        pl.semaphore_signal(here_sem, inc=1, device_id=neighbour, device_id_type=MESH)
+    @pl.when(is_hub)
+    def _():
+        pl.semaphore_wait(barrier, 4)
+        for other in (neighbour, sibling, {**neighbour, **sibling}):
+            pl.semaphore_signal(here_sem, inc=1, device_id=other, device_id_type=MESH)
 
     def start_a(tiles):
         for m in tiles:
@@ -159,9 +148,9 @@
     early, late = range(2), range(2, TILES)
     start_a(early)
 
-    @pl.when(root)
-    def _():
-        pl.semaphore_wait(here_sem, 2)
+    @pl.when(jnp.logical_not(is_hub))
+    def _():
+        pl.semaphore_wait(here_sem, 1)
 
     for t in range(AHEAD):
         send_b(0, t).start()

time: 1270 us -> 1270 us (level)
  no operation moved by 1% of the time
where the time goes in v7:
time: 1270 us; the launch traced here: 1260 us
  Pallas kernels  1220 us (96%)
  waiting for transfers between devices  28.6 us (2%)
    pallas_call x1, Pallas kernels, device_product(): pl.pallas_call(functools.partial(kernel, n_blocks, tile), out_shape=(jax....  1210 us
    ppermute x1, waiting for transfers between devices, device_product(): got_early = lax.ppermute(p_early, 'row', swap)  28.6 us
  transfers between devices with their start and end apart: 2, of which 1 were waited for; matrix products, arithmetic and copies ran while one was open for 0% of the time, Pallas kernels for 1%

profile of v7, /device:TPU:0, one launch (start us, length us, event | category | flops | bytes accessed | tf_op | source)
XLA Modules:
  0.0 1257.4 jit_solution(10355547148245518339)
XLA Ops:
  0.0 1209.0 %split_sum_product.1 = (bf16[1024,10240]{1,0:T(8,128)(2,1)}, f32[19,1024,512]{2,1,0:T(8,128)}, f32[896,512]{1,0:T(8,128)}, f32[128,512]{1,0:T(8,128)}, f32[896,5...) custom-call(bf16[1024,16384]{1,0:T(8,128)(2,1)} %a_ref.1, ...), custom_call_target="tpu_custom_call" | custom-call | tf_op jit(solution)/shard_map/split_sum_product/pallas_call | solution.py:369
  1209.0 2.0 collective-permute-start.1
  1211.1 0.0 collective-permute-start
  1211.1 0.0 copy-start
  1211.1 0.0 copy-start.1
  1211.1 14.2 %write_out.1 = bf16[1024,10240]{1,0:T(8,128)(2,1)} custom-call(bf16[1024,10240]{1,0:T(8,128)(2,1)} %get-tuple-element.12.c_ref, f32[1024,512]{1,0:T(8,128)} %get-tuple-element.13.q_ref, f32[19,1024,512]{2,1,0:T(8,128)} %get-tuple-element.14.r_ref), custom_call_target="tpu_custom_call" | custom-call | flops 20000000000 | bytes 41943040 | tf_op jit(solution)/shard_map/write_out/pallas_call | solution.py:415
  1225.3 28.6 %collective-permute-done = f32[896,512]{1,0:T(8,128)} collective-permute-done((f32[896,512]{1,0:T(8,128)}, f32[896,512]{1,0:T(8,128)}, u32[]{:S(2)}, u32[]{:S(2)}) %collective-permute-start) | collective-permute-done | bytes 1835040 | tf_op jit(solution)/shard_map/ppermute | solution.py:413
  1253.9 0.0 copy-done
  1253.9 2.7 fusion
  1256.7 0.0 collective-permute-done.1
  1256.7 0.0 copy-done.1
  1256.7 0.7 fusion.1
Async XLA Ops:
  1209.0 47.6 %collective-permute-start.1 = (f32[128,512]{1,0:T(8,128)}, f32[128,512]{1,0:T(8,128)S(1)}, u32[]{:S(2)}, u32[]{:S(2)}) collective-permute-start(f32[128,512]{1,0:T(8,128)} %get-tuple-element.18), channel_id=1, source_target_pairs={{0,2},{2,0},{1,3},{3,1},{4,6},{6,4},{5,7},{7,5}} | collective-permute-start | bytes 786440 | tf_op jit(solution)/shard_map/ppermute | solution.py:414
  1211.1 42.9 %collective-permute-start = (f32[896,512]{1,0:T(8,128)}, f32[896,512]{1,0:T(8,128)}, u32[]{:S(2)}, u32[]{:S(2)}) collective-permute-start(f32[896,512]{1,0:T(8,128)} %get-tuple-element.16), channel_id=1, source_target_pairs={{0,2},{2,0},{1,3},{3,1},{4,6},{6,4},{5,7},{7,5}} | collective-permute-start | bytes 5505032 | tf_op jit(solution)/shard_map/ppermute | solution.py:413
  1211.1 42.8 %copy-start = (f32[896,512]{1,0:T(8,128)S(1)}, f32[896,512]{1,0:T(8,128)}, u32[]{:S(2)}) copy-start(f32[896,512]{1,0:T(8,128)} %get-tuple-element.15) | copy-start | bytes 5505028
  1211.1 45.6 %copy-start.1 = (f32[128,512]{1,0:T(8,128)S(1)}, f32[128,512]{1,0:T(8,128)}, u32[]{:S(2)}) copy-start(f32[128,512]{1,0:T(8,128)} %get-tuple-element.17) | copy-start | bytes 786436

commit v8 on v7

--- a/solution.py
+++ b/solution.py
@@ -13,17 +13,18 @@
 TILES = 4
 AHEAD = 4
 SLOTS = 3
-LATE = 128
+PARTS = (8, 6, 2)
 HUB = (1, 0)
-PIECES = 2
+PIECES = 1
 RING = 2 * (SLOTS + 1)
 
 
 def kernel(
-    n_blocks, tile, a_ref, b_ref, c_ref, r_got, p_early, p_late, q_early, q_late, q_done, b_got,
-    a_buf, b_buf, p_buf, q_buf, r_buf, c_buf,
-    a_own_sem, a_send, a_recv, b_send, b_recv, b_load_sem, first_send, first_recv, p_send, r_recv, r_load_sem, c_sem, q_sem, last_sem, here_sem,
+    n_blocks, tile, a_ref, b_ref, c_ref, r_got, q_done, b_got, *rest,
 ):
+    p_parts, q_parts, rest = rest[: len(PARTS)], rest[len(PARTS) : 2 * len(PARTS)], rest[2 * len(PARTS) :]
+    (a_buf, b_buf, p_buf, q_buf, r_buf, c_buf,
+    a_own_sem, a_send, a_recv, b_send, b_recv, b_load_sem, first_send, first_recv, p_send, r_recv, r_load_sem, c_sem, q_sem, last_sem, here_sem) = rest
     last = n_blocks - 1
     col, row, core = lax.axis_index("col"), lax.axis_index("row"), lax.axis_index("depth")
     neighbour, partner, sibling = {"col": 1 - col}, {"row": 1 - row}, {"depth": 1 - core}
@@ -80,7 +81,8 @@
     def store_c(q):
         return pltpu.make_async_copy(c_buf, c_ref.at[:, cols_of(q)], c_sem)
 
-    parts = (pl.ds(0, p_early.shape[0]), pl.ds(p_early.shape[0], p_late.shape[0]))
+    sixteenth = p_buf.shape[1] // sum(PARTS)
+    parts = [pl.ds(sum(PARTS[:i]) * sixteenth, n * sixteenth) for i, n in enumerate(PARTS)]
 
     def store_q_done():
         return pltpu.make_async_copy(q_buf, q_done, q_sem.at[0])
@@ -88,13 +90,13 @@
     def store_q():
         return [
             pltpu.make_async_copy(q_buf.at[part], out, q_sem.at[i])
-            for i, (part, out) in enumerate(zip(parts, (q_early, q_late)))
+            for i, (part, out) in enumerate(zip(parts, q_parts))
         ]
 
     def store_p():
         return [
             pltpu.make_async_copy(p_buf.at[last % SLOTS, part], out, last_sem.at[i])
-            for i, (part, out) in enumerate(zip(parts, (p_early, p_late)))
+            for i, (part, out) in enumerate(zip(parts, p_parts))
         ]
 
     def product(whose, m, slot):
@@ -343,10 +345,10 @@
     load_q = pltpu.make_async_copy(q_ref, q_buf, load_sem.at[PIECES])
     load_r = pltpu.make_async_copy(r_ref.at[r_ref.shape[0] - 1], r_buf, load_sem.at[PIECES + 1])
     store_sum = pltpu.make_async_copy(o_buf, out_ref.at[:, pl.ds(done, o_buf.shape[1])], store_sem.at[PIECES])
+    load_q.start()
+    load_r.start()
     for i in range(PIECES):
         load(i).start()
-    load_q.start()
-    load_r.start()
     for i in range(PIECES):
         load(i).wait()
         store(i).start()
@@ -362,24 +364,23 @@
 def device_product(block, a_rows, b_rows):
     rows, _ = a_rows.shape
     depth, n_cols = b_rows.shape
-    n_blocks, tile, early = n_cols // block, rows // TILES, rows - LATE
+    n_blocks, tile, sixteenth = n_cols // block, rows // TILES, rows // sum(PARTS)
     last = n_blocks - 1
     anywhere = pl.BlockSpec(memory_space=pl.ANY)
     dma = pltpu.SemaphoreType.DMA
-    c_main, r_got, p_early, p_late, q_early, q_late, q_done, _ = pl.pallas_call(
+    parts = [jax.ShapeDtypeStruct((n * sixteenth, block), jnp.float32) for n in PARTS]
+    c_main, r_got, q_done, _, *rest = pl.pallas_call(
         functools.partial(kernel, n_blocks, tile),
         out_shape=(
             jax.ShapeDtypeStruct((rows, n_cols), jnp.bfloat16),
             jax.ShapeDtypeStruct((last, rows, block), jnp.float32),
-            jax.ShapeDtypeStruct((early, block), jnp.float32),
-            jax.ShapeDtypeStruct((LATE, block), jnp.float32),
-            jax.ShapeDtypeStruct((early, block), jnp.float32),
-            jax.ShapeDtypeStruct((LATE, block), jnp.float32),
             jax.ShapeDtypeStruct((rows, block), jnp.float32),
             jax.ShapeDtypeStruct((3, n_blocks, depth, block), jnp.bfloat16),
+            *parts,
+            *parts,
         ),
         in_specs=[anywhere] * 2,
-        out_specs=(anywhere,) * 8,
+        out_specs=(anywhere,) * (4 + 2 * len(PARTS)),
         scratch_shapes=[
             pltpu.VMEM((2, rows, 4 * depth), jnp.bfloat16),
             pltpu.VMEM((2, 4 * depth, block), jnp.bfloat16),
@@ -399,8 +400,8 @@
             dma((RING,)),
             dma,
             dma,
-            dma((2,)),
-            dma((2,)),
+            dma((len(PARTS),)),
+            dma((len(PARTS),)),
             pltpu.SemaphoreType.REGULAR,
         ],
         compiler_params=pltpu.CompilerParams(
@@ -409,9 +410,10 @@
         name="split_sum_product",
     )(a_rows, b_rows)
 
-    swap = [(0, 1), (1, 0)]
-    got_early = lax.ppermute(p_early, "row", swap)
-    got_late = lax.ppermute(p_late, "row", swap)
+    p_parts, q_parts = rest[: len(PARTS)], rest[len(PARTS) :]
+    got = []
+    for part in p_parts:
+        got.append(lax.ppermute(part, "row", [(0, 1), (1, 0)]))
     out = pl.pallas_call(
         write_out,
         out_shape=jax.ShapeDtypeStruct((rows, n_cols), jnp.bfloat16),
@@ -428,7 +430,8 @@
         cost_estimate=pl.CostEstimate(flops=20_000_000_000, bytes_accessed=4 * rows * n_cols, transcendentals=0),
         name="write_out",
     )(c_main, q_done, r_got)
-    for start, own, part in ((0, q_early, got_early), (early, q_late, got_late)):
+    for i, (own, part) in enumerate(zip(q_parts, got)):
+        start = sum(PARTS[:i]) * sixteenth
         out = lax.dynamic_update_slice(out, (own + part).astype(out.dtype), (start, last * block))
     return out
 

time: 1270 us -> 1270 us (level)
    ppermute x2 -> x3, waiting for transfers between devices: 28.6 us -> 25.7 us  [device_product(): got.append(lax.ppermute(part, 'row', [(0, 1), (1, 0)]))]
  transfers between devices with their start and end apart: 2 -> 3, of which waited for: 1 -> 1; matrix products, arithmetic and copies ran while one was open for 0% -> 0% of each run, Pallas kernels for 1% -> 1%
where the time goes in v8:
time: 1270 us; the launch traced here: 1260 us
  Pallas kernels  1220 us (96%)
  waiting for transfers between devices  25.7 us (2%)
    pallas_call x1, Pallas kernels, device_product(): pl.pallas_call(functools.partial(kernel, n_blocks, tile), out_shape=(jax....  1210 us
    ppermute x3, waiting for transfers between devices, device_product(): got.append(lax.ppermute(part, 'row', [(0, 1), (1, 0)]))  25.7 us
  transfers between devices with their start and end apart: 3, of which 1 were waited for; matrix products, arithmetic and copies ran while one was open for 0% of the time, Pallas kernels for 1%

profile of v8, /device:TPU:0, one launch (start us, length us, event | category | flops | bytes accessed | tf_op | source)
XLA Modules:
  0.0 1257.5 jit_solution(17211523965674241019)
XLA Ops:
  0.0 1209.0 %split_sum_product.1 = (bf16[1024,10240]{1,0:T(8,128)(2,1)}, f32[19,1024,512]{2,1,0:T(8,128)}, f32[1024,512]{1,0:T(8,128)}, bf16[3,20,2048,512]{3,2,1,0:T(8,128)...) custom-call(bf16[1024,16384]{1,0:T(8,128)(2,1)} %a_ref.1, ...), custom_call_target="tpu_custom_call" | custom-call | tf_op jit(solution)/shard_map/split_sum_product/pallas_call | solution.py:372
  1209.1 2.0 collective-permute-start.2
  1211.1 0.0 collective-permute-start.1
  1211.1 2.0 collective-permute-start
  1213.1 0.0 copy-start
  1213.1 0.0 copy-start.1
  1213.1 0.0 copy-start.2
  1213.1 15.0 %write_out.1 = bf16[1024,10240]{1,0:T(8,128)(2,1)} custom-call(bf16[1024,10240]{1,0:T(8,128)(2,1)} %get-tuple-element.14.c_ref, f32[1024,512]{1,0:T(8,128)} %get-tuple-element.15.q_ref, f32[19,1024,512]{2,1,0:T(8,128)} %get-tuple-element.16.r_ref), custom_call_target="tpu_custom_call" | custom-call | flops 20000000000 | bytes 41943040 | tf_op jit(solution)/shard_map/write_out/pallas_call | solution.py:417
  1228.1 25.7 %collective-permute-done = f32[512,512]{1,0:T(8,128)S(1)} collective-permute-done((f32[512,512]{1,0:T(8,128)}, f32[512,512]{1,0:T(8,128)S(1)}, u32[]{:S(2)}, u32[]{:S(2)}) %collective-permute-start) | collective-permute-done | bytes 1048608 | tf_op jit(solution)/shard_map/ppermute | solution.py:416
  1253.8 0.0 copy-done
  1253.8 0.9 fusion
  1254.8 0.0 collective-permute-done.1
  1254.8 0.0 copy-done.1
  1254.8 2.0 fusion.1
  1256.8 0.0 collective-permute-done.2
  1256.8 0.0 copy-done.2
  1256.8 0.7 fusion.2
Async XLA Ops:
  1209.1 47.7 %collective-permute-start.2 = (f32[128,512]{1,0:T(8,128)}, f32[128,512]{1,0:T(8,128)S(1)}, u32[]{:S(2)}, u32[]{:S(2)}) collective-permute-start(f32[128,512]{1,0:T(8,128)} %get-tuple-element.22), channel_id=1, source_target_pairs={{0,2},{2,0},{1,3},{3,1},{4,6},{6,4},{5,7},{7,5}} | collective-permute-start | bytes 786440 | tf_op jit(solution)/shard_map/ppermute | solution.py:416
  1211.1 43.7 %collective-permute-start.1 = (f32[384,512]{1,0:T(8,128)}, f32[384,512]{1,0:T(8,128)}, u32[]{:S(2)}, u32[]{:S(2)}) collective-permute-start(f32[384,512]{1,0:T(8,128)} %get-tuple-element.20), channel_id=1, source_target_pairs={{0,2},{2,0},{1,3},{3,1},{4,6},{6,4},{5,7},{7,5}} | collective-permute-start | bytes 2359304 | tf_op jit(solution)/shard_map/ppermute | solution.py:416
  1211.1 42.7 %collective-permute-start = (f32[512,512]{1,0:T(8,128)}, f32[512,512]{1,0:T(8,128)S(1)}, u32[]{:S(2)}, u32[]{:S(2)}) collective-permute-start(f32[512,512]{1,0:T(8,128)} %get-tuple-element.18), channel_id=1, source_target_pairs={{0,2},{2,0},{1,3},{3,1},{4,6},{6,4},{5,7},{7,5}} | collective-permute-start | bytes 3145736 | tf_op jit(solution)/shard_map/ppermute | solution.py:416
  1213.1 40.7 %copy-start = (f32[512,512]{1,0:T(8,128)S(1)}, f32[512,512]{1,0:T(8,128)}, u32[]{:S(2)}) copy-start(f32[512,512]{1,0:T(8,128)} %get-tuple-element.17) | copy-start | bytes 3145732
  1213.1 41.7 %copy-start.1 = (f32[384,512]{1,0:T(8,128)S(1)}, f32[384,512]{1,0:T(8,128)}, u32[]{:S(2)}) copy-start(f32[384,512]{1,0:T(8,128)} %get-tuple-element.19) | copy-start | bytes 2359300
  1213.1 43.7 %copy-start.2 = (f32[128,512]{1,0:T(8,128)S(1)}, f32[128,512]{1,0:T(8,128)}, u32[]{:S(2)}) copy-start(f32[128,512]{1,0:T(8,128)} %get-tuple-element.21) | copy-start | bytes 786436

commit v9 on v7

--- a/solution.py
+++ b/solution.py
@@ -15,14 +15,16 @@
 SLOTS = 3
 LATE = 128
 HUB = (1, 0)
+SLAB = 16
+ROUND = 8
 PIECES = 2
 RING = 2 * (SLOTS + 1)
 
 
 def kernel(
-    n_blocks, tile, a_ref, b_ref, c_ref, r_got, p_early, p_late, q_early, q_late, q_done, b_got,
+    n_blocks, tile, a_ref, b_ref, c_ref, r_got, p_early, p_late, q_early, q_late, q_done, b_got, relay,
     a_buf, b_buf, p_buf, q_buf, r_buf, c_buf,
-    a_own_sem, a_send, a_recv, b_send, b_recv, b_load_sem, first_send, first_recv, p_send, r_recv, r_load_sem, c_sem, q_sem, last_sem, here_sem,
+    a_own_sem, a_send, a_recv, b_send, b_recv, b_load_sem, first_send, first_recv, p_send, r_recv, r_load_sem, c_sem, q_sem, last_sem, here_sem, hop_send, hop_recv,
 ):
     last = n_blocks - 1
     col, row, core = lax.axis_index("col"), lax.axis_index("row"), lax.axis_index("depth")
@@ -74,6 +76,23 @@
             src_ref=p_buf.at[lax.rem(s, SLOTS)], dst_ref=r_got.at[s],
             send_sem=p_send.at[lax.rem(s, SLOTS)], recv_sem=r_recv.at[lax.rem(s, RING)], device_id=partner, device_id_type=MESH)
 
+    slab, rest = pl.ds(0, SLAB), pl.ds(SLAB, p_buf.shape[1] - SLAB)
+
+    def at(c, r):
+        return jnp.logical_and(core == 1, jnp.logical_and(col == c, row == r))
+
+    def send_rest():
+        return pltpu.make_async_remote_copy(
+            src_ref=p_buf.at[ROUND % SLOTS, rest], dst_ref=r_got.at[ROUND, rest],
+            send_sem=p_send.at[ROUND % SLOTS], recv_sem=r_recv.at[ROUND % RING], device_id=partner, device_id_type=MESH)
+
+    def hop(i):
+        sources = (p_buf.at[ROUND % SLOTS, slab], relay.at[0], relay.at[1])
+        targets = (relay.at[0], relay.at[1], r_got.at[ROUND, slab])
+        return pltpu.make_async_remote_copy(
+            src_ref=sources[i], dst_ref=targets[i], send_sem=hop_send.at[i], recv_sem=hop_recv.at[i],
+            device_id=partner if i == 1 else neighbour, device_id_type=MESH)
+
     def load_r(q):
         return pltpu.make_async_copy(r_got.at[q], r_buf, r_load_sem)
 
@@ -204,9 +223,16 @@
                 for m in range(TILES):
                     send_first(m).wait_send()
 
-            @pl.when(s > SLOTS)
+            slab_sent = jnp.logical_and(s == ROUND + SLOTS, at(0, 1))
+
+            @pl.when(jnp.logical_and(s > SLOTS, jnp.logical_not(slab_sent)))
             def _():
                 send_block(s - SLOTS).wait_send()
+
+            @pl.when(slab_sent)
+            def _():
+                send_rest().wait_send()
+                hop(0).wait_send()
 
             @pl.loop(0, TILES)
             def _(m):
@@ -226,9 +252,22 @@
                 for copy in store_p():
                     copy.start()
 
-            @pl.when(jnp.logical_and(s > 0, s < last))
+            slab_goes = jnp.logical_and(s == ROUND, at(0, 1))
+
+            @pl.when(jnp.logical_and(jnp.logical_and(s > 0, s < last), jnp.logical_not(slab_goes)))
             def _():
                 send_block(s).start()
+
+            @pl.when(slab_goes)
+            def _():
+                send_rest().start()
+                hop(0).start()
+
+            for i, place in ((1, (1, 1)), (2, (1, 0))):
+                @pl.when(jnp.logical_and(s == ROUND + i, at(*place)))
+                def _():
+                    hop(i - 1).wait_recv()
+                    hop(i).start()
 
             @pl.when(s + AHEAD < n_blocks)
             def _():
@@ -247,9 +286,16 @@
                 for m in range(TILES):
                     send_first(m).wait_recv()
 
-            @pl.when(jnp.logical_and(q > 0, q < last - 1))
+            slab_comes = jnp.logical_and(q == ROUND, at(0, 0))
+
+            @pl.when(jnp.logical_and(jnp.logical_and(q > 0, q < last - 1), jnp.logical_not(slab_comes)))
             def _():
                 send_block(q).wait_recv()
+
+            @pl.when(slab_comes)
+            def _():
+                send_rest().wait_recv()
+                hop(2).wait_recv()
 
             @pl.when(q < last - 1)
             def _():
@@ -308,6 +354,11 @@
         @pl.when(t >= n_blocks - RING + AHEAD)
         def _():
             send_b(0, t).wait_send()
+
+    for i, place in ((1, (1, 1)), (2, (1, 0))):
+        @pl.when(at(*place))
+        def _():
+            hop(i).wait_send()
 
     store_c(last - 2).wait()
     for copy in store_q() + store_p():
@@ -366,7 +417,7 @@
     last = n_blocks - 1
     anywhere = pl.BlockSpec(memory_space=pl.ANY)
     dma = pltpu.SemaphoreType.DMA
-    c_main, r_got, p_early, p_late, q_early, q_late, q_done, _ = pl.pallas_call(
+    c_main, r_got, p_early, p_late, q_early, q_late, q_done, _, _ = pl.pallas_call(
         functools.partial(kernel, n_blocks, tile),
         out_shape=(
             jax.ShapeDtypeStruct((rows, n_cols), jnp.bfloat16),
@@ -377,9 +428,10 @@
             jax.ShapeDtypeStruct((LATE, block), jnp.float32),
             jax.ShapeDtypeStruct((rows, block), jnp.float32),
             jax.ShapeDtypeStruct((3, n_blocks, depth, block), jnp.bfloat16),
+            jax.ShapeDtypeStruct((2, SLAB, block), jnp.float32),
         ),
         in_specs=[anywhere] * 2,
-        out_specs=(anywhere,) * 8,
+        out_specs=(anywhere,) * 9,
         scratch_shapes=[
             pltpu.VMEM((2, rows, 4 * depth), jnp.bfloat16),
             pltpu.VMEM((2, 4 * depth, block), jnp.bfloat16),
@@ -402,6 +454,8 @@
             dma((2,)),
             dma((2,)),
             pltpu.SemaphoreType.REGULAR,
+            dma((3,)),
+            dma((3,)),
         ],
         compiler_params=pltpu.CompilerParams(
             collective_id=0, has_side_effects=True, vmem_limit_bytes=66_000_000

time: 1270 us -> 1260 us (level)
  no operation moved by 1% of the time
where the time goes in v9:
time: 1260 us
  Pallas kernels  1220 us (97%)
  waiting for transfers between devices  28.1 us (2%)
    pallas_call x1, Pallas kernels, device_product(): pl.pallas_call(functools.partial(kernel, n_blocks, tile), out_shape=(jax....  1210 us
    ppermute x1, waiting for transfers between devices, device_product(): got_early = lax.ppermute(p_early, 'row', swap)  28.1 us
  transfers between devices with their start and end apart: 2, of which 1 were waited for; matrix products, arithmetic and copies ran while one was open for 0% of the time, Pallas kernels for 1%

profile of v9, /device:TPU:0, one launch (start us, length us, event | category | flops | bytes accessed | tf_op | source)
XLA Modules:
  0.0 1256.9 jit_solution(17954510306774003896)
XLA Ops:
  0.0 1209.1 %split_sum_product.1 = (bf16[1024,10240]{1,0:T(8,128)(2,1)}, f32[19,1024,512]{2,1,0:T(8,128)}, f32[896,512]{1,0:T(8,128)}, f32[128,512]{1,0:T(8,128)}, f32[896,5...) custom-call(bf16[1024,16384]{1,0:T(8,128)(2,1)} %a_ref.1, ...), custom_call_target="tpu_custom_call" | custom-call | tf_op jit(solution)/shard_map/split_sum_product/pallas_call | solution.py:420
  1209.1 2.0 collective-permute-start.1
  1211.1 0.0 collective-permute-start
  1211.1 0.0 copy-start
  1211.1 0.0 copy-start.1
  1211.1 14.2 %write_out.1 = bf16[1024,10240]{1,0:T(8,128)(2,1)} custom-call(bf16[1024,10240]{1,0:T(8,128)(2,1)} %get-tuple-element.12.c_ref, f32[1024,512]{1,0:T(8,128)} %get-tuple-element.13.q_ref, f32[19,1024,512]{2,1,0:T(8,128)} %get-tuple-element.14.r_ref), custom_call_target="tpu_custom_call" | custom-call | flops 20000000000 | bytes 41943040 | tf_op jit(solution)/shard_map/write_out/pallas_call | solution.py:469
  1225.4 28.1 %collective-permute-done = f32[896,512]{1,0:T(8,128)} collective-permute-done((f32[896,512]{1,0:T(8,128)}, f32[896,512]{1,0:T(8,128)}, u32[]{:S(2)}, u32[]{:S(2)}) %collective-permute-start) | collective-permute-done | bytes 1835040 | tf_op jit(solution)/shard_map/ppermute | solution.py:467
  1253.5 0.0 copy-done
  1253.5 2.7 fusion
  1256.2 0.0 collective-permute-done.1
  1256.2 0.0 copy-done.1
  1256.2 0.7 fusion.1
Async XLA Ops:
  1209.1 47.1 %collective-permute-start.1 = (f32[128,512]{1,0:T(8,128)}, f32[128,512]{1,0:T(8,128)S(1)}, u32[]{:S(2)}, u32[]{:S(2)}) collective-permute-start(f32[128,512]{1,0:T(8,128)} %get-tuple-element.18), channel_id=1, source_target_pairs={{0,2},{2,0},{1,3},{3,1},{4,6},{6,4},{5,7},{7,5}} | collective-permute-start | bytes 786440 | tf_op jit(solution)/shard_map/ppermute | solution.py:468
  1211.1 42.4 %collective-permute-start = (f32[896,512]{1,0:T(8,128)}, f32[896,512]{1,0:T(8,128)}, u32[]{:S(2)}, u32[]{:S(2)}) collective-permute-start(f32[896,512]{1,0:T(8,128)} %get-tuple-element.16), channel_id=1, source_target_pairs={{0,2},{2,0},{1,3},{3,1},{4,6},{6,4},{5,7},{7,5}} | collective-permute-start | bytes 5505032 | tf_op jit(solution)/shard_map/ppermute | solution.py:467
  1211.1 42.3 %copy-start = (f32[896,512]{1,0:T(8,128)S(1)}, f32[896,512]{1,0:T(8,128)}, u32[]{:S(2)}) copy-start(f32[896,512]{1,0:T(8,128)} %get-tuple-element.15) | copy-start | bytes 5505028
  1211.1 45.1 %copy-start.1 = (f32[128,512]{1,0:T(8,128)S(1)}, f32[128,512]{1,0:T(8,128)}, u32[]{:S(2)}) copy-start(f32[128,512]{1,0:T(8,128)} %get-tuple-element.17) | copy-start | bytes 786436

commit v10 on v9

--- a/solution.py
+++ b/solution.py
@@ -13,19 +13,23 @@
 TILES = 4
 AHEAD = 4
 SLOTS = 3
-LATE = 128
+PARTS = (16, 12, 3, 1)
 HUB = (1, 0)
 SLAB = 16
 ROUND = 8
-PIECES = 2
+PIECES = 1
 RING = 2 * (SLOTS + 1)
 
 
 def kernel(
-    n_blocks, tile, a_ref, b_ref, c_ref, r_got, p_early, p_late, q_early, q_late, q_done, b_got, relay,
-    a_buf, b_buf, p_buf, q_buf, r_buf, c_buf,
-    a_own_sem, a_send, a_recv, b_send, b_recv, b_load_sem, first_send, first_recv, p_send, r_recv, r_load_sem, c_sem, q_sem, last_sem, here_sem, hop_send, hop_recv,
+    n_blocks, tile, a_ref, b_ref, c_ref, r_got, q_done, b_got, relay, *others,
 ):
+    p_parts, q_parts, scratch = others[: len(PARTS)], others[len(PARTS) : 2 * len(PARTS)], others[2 * len(PARTS) :]
+    (
+        a_buf, b_buf, p_buf, q_buf, r_buf, c_buf,
+        a_own_sem, a_send, a_recv, b_send, b_recv, b_load_sem, first_send, first_recv, p_send, r_recv,
+        r_load_sem, c_sem, q_sem, last_sem, here_sem, hop_send, hop_recv,
+    ) = scratch
     last = n_blocks - 1
     col, row, core = lax.axis_index("col"), lax.axis_index("row"), lax.axis_index("depth")
     neighbour, partner, sibling = {"col": 1 - col}, {"row": 1 - row}, {"depth": 1 - core}
@@ -99,7 +103,8 @@
     def store_c(q):
         return pltpu.make_async_copy(c_buf, c_ref.at[:, cols_of(q)], c_sem)
 
-    parts = (pl.ds(0, p_early.shape[0]), pl.ds(p_early.shape[0], p_late.shape[0]))
+    unit = p_buf.shape[1] // sum(PARTS)
+    parts = [pl.ds(sum(PARTS[:i]) * unit, n * unit) for i, n in enumerate(PARTS)]
 
     def store_q_done():
         return pltpu.make_async_copy(q_buf, q_done, q_sem.at[0])
@@ -107,13 +112,13 @@
     def store_q():
         return [
             pltpu.make_async_copy(q_buf.at[part], out, q_sem.at[i])
-            for i, (part, out) in enumerate(zip(parts, (q_early, q_late)))
+            for i, (part, out) in enumerate(zip(parts, q_parts))
         ]
 
     def store_p():
         return [
             pltpu.make_async_copy(p_buf.at[last % SLOTS, part], out, last_sem.at[i])
-            for i, (part, out) in enumerate(zip(parts, (p_early, p_late)))
+            for i, (part, out) in enumerate(zip(parts, p_parts))
         ]
 
     def product(whose, m, slot):
@@ -394,10 +399,10 @@
     load_q = pltpu.make_async_copy(q_ref, q_buf, load_sem.at[PIECES])
     load_r = pltpu.make_async_copy(r_ref.at[r_ref.shape[0] - 1], r_buf, load_sem.at[PIECES + 1])
     store_sum = pltpu.make_async_copy(o_buf, out_ref.at[:, pl.ds(done, o_buf.shape[1])], store_sem.at[PIECES])
+    load_q.start()
+    load_r.start()
     for i in range(PIECES):
         load(i).start()
-    load_q.start()
-    load_r.start()
     for i in range(PIECES):
         load(i).wait()
         store(i).start()
@@ -413,25 +418,24 @@
 def device_product(block, a_rows, b_rows):
     rows, _ = a_rows.shape
     depth, n_cols = b_rows.shape
-    n_blocks, tile, early = n_cols // block, rows // TILES, rows - LATE
+    n_blocks, tile, unit = n_cols // block, rows // TILES, rows // sum(PARTS)
     last = n_blocks - 1
     anywhere = pl.BlockSpec(memory_space=pl.ANY)
     dma = pltpu.SemaphoreType.DMA
-    c_main, r_got, p_early, p_late, q_early, q_late, q_done, _, _ = pl.pallas_call(
+    parts = [jax.ShapeDtypeStruct((n * unit, block), jnp.float32) for n in PARTS]
+    c_main, r_got, q_done, _, _, *split = pl.pallas_call(
         functools.partial(kernel, n_blocks, tile),
         out_shape=(
             jax.ShapeDtypeStruct((rows, n_cols), jnp.bfloat16),
             jax.ShapeDtypeStruct((last, rows, block), jnp.float32),
-            jax.ShapeDtypeStruct((early, block), jnp.float32),
-            jax.ShapeDtypeStruct((LATE, block), jnp.float32),
-            jax.ShapeDtypeStruct((early, block), jnp.float32),
-            jax.ShapeDtypeStruct((LATE, block), jnp.float32),
             jax.ShapeDtypeStruct((rows, block), jnp.float32),
             jax.ShapeDtypeStruct((3, n_blocks, depth, block), jnp.bfloat16),
             jax.ShapeDtypeStruct((2, SLAB, block), jnp.float32),
+            *parts,
+            *parts,
         ),
         in_specs=[anywhere] * 2,
-        out_specs=(anywhere,) * 9,
+        out_specs=(anywhere,) * (5 + 2 * len(PARTS)),
         scratch_shapes=[
             pltpu.VMEM((2, rows, 4 * depth), jnp.bfloat16),
             pltpu.VMEM((2, 4 * depth, block), jnp.bfloat16),
@@ -451,8 +455,8 @@
             dma((RING,)),
             dma,
             dma,
-            dma((2,)),
-            dma((2,)),
+            dma((len(PARTS),)),
+            dma((len(PARTS),)),
             pltpu.SemaphoreType.REGULAR,
             dma((3,)),
             dma((3,)),
@@ -463,9 +467,10 @@
         name="split_sum_product",
     )(a_rows, b_rows)
 
-    swap = [(0, 1), (1, 0)]
-    got_early = lax.ppermute(p_early, "row", swap)
-    got_late = lax.ppermute(p_late, "row", swap)
+    p_parts, q_parts = split[: len(PARTS)], split[len(PARTS) :]
+    got = []
+    for part in p_parts:
+        got.append(lax.ppermute(part, "row", [(0, 1), (1, 0)]))
     out = pl.pallas_call(
         write_out,
         out_shape=jax.ShapeDtypeStruct((rows, n_cols), jnp.bfloat16),
@@ -482,7 +487,8 @@
         cost_estimate=pl.CostEstimate(flops=20_000_000_000, bytes_accessed=4 * rows * n_cols, transcendentals=0),
         name="write_out",
     )(c_main, q_done, r_got)
-    for start, own, part in ((0, q_early, got_early), (early, q_late, got_late)):
+    for i, (own, part) in enumerate(zip(q_parts, got)):
+        start = sum(PARTS[:i]) * unit
         out = lax.dynamic_update_slice(out, (own + part).astype(out.dtype), (start, last * block))
     return out
 

time: 1260 us -> 1270 us (level)
    ppermute x2 -> x4, waiting for transfers between devices: 28.1 us -> 25.2 us  [device_product(): got.append(lax.ppermute(part, 'row', [(0, 1), (1, 0)]))]
  transfers between devices with their start and end apart: 2 -> 4, of which waited for: 1 -> 1; matrix products, arithmetic and copies ran while one was open for 0% -> 0% of each run, Pallas kernels for 1% -> 1%
where the time goes in v10:
time: 1270 us; the launch traced here: 1260 us
  Pallas kernels  1220 us (96%)
  waiting for transfers between devices  25.2 us (2%)
    pallas_call x1, Pallas kernels, device_product(): pl.pallas_call(functools.partial(kernel, n_blocks, tile), out_shape=(jax....  1210 us
  transfers between devices with their start and end apart: 4, of which 1 were waited for; matrix products, arithmetic and copies ran while one was open for 0% of the time, Pallas kernels for 1%

profile of v10, /device:TPU:0, one launch (start us, length us, event | category | flops | bytes accessed | tf_op | source)
XLA Modules:
  0.0 1257.7 jit_solution(7656038608017532292)
XLA Ops:
  0.0 1209.1 %split_sum_product.1 = (bf16[1024,10240]{1,0:T(8,128)(2,1)}, f32[19,1024,512]{2,1,0:T(8,128)}, f32[1024,512]{1,0:T(8,128)}, bf16[3,20,2048,512]{3,2,1,0:T(8,128)...) custom-call(bf16[1024,16384]{1,0:T(8,128)(2,1)} %a_ref.1, ...), custom_call_target="tpu_custom_call" | custom-call | tf_op jit(solution)/shard_map/split_sum_product/pallas_call | solution.py:426
  1209.1 2.0 collective-permute-start.3
  1211.1 0.0 collective-permute-start.2
  1211.2 2.0 collective-permute-start.1
  1213.2 0.0 collective-permute-start
  1213.2 0.0 copy-start
  1213.2 0.0 copy-start.1
  1213.2 0.0 copy-start.2
  1213.2 0.0 copy-start.3
  1213.2 15.0 %write_out.1 = bf16[1024,10240]{1,0:T(8,128)(2,1)} custom-call(bf16[1024,10240]{1,0:T(8,128)(2,1)} %get-tuple-element.16.c_ref, f32[1024,512]{1,0:T(8,128)} %get-tuple-element.17.q_ref, f32[19,1024,512]{2,1,0:T(8,128)} %get-tuple-element.18.r_ref), custom_call_target="tpu_custom_call" | custom-call | flops 20000000000 | bytes 41943040 | tf_op jit(solution)/shard_map/write_out/pallas_call | solution.py:474
  1228.2 25.2 %collective-permute-done = f32[512,512]{1,0:T(8,128)S(1)} collective-permute-done((f32[512,512]{1,0:T(8,128)}, f32[512,512]{1,0:T(8,128)S(1)}, u32[]{:S(2)}, u32[]{:S(2)}) %collective-permute-start) | collective-permute-done | bytes 1048608 | tf_op jit(solution)/shard_map/ppermute | solution.py:473
  1253.4 0.0 copy-done
  1253.5 0.9 fusion
  1254.4 0.0 collective-permute-done.1
  1254.4 0.0 copy-done.1
  1254.4 2.0 fusion.1
  1256.4 0.0 collective-permute-done.2
  1256.4 0.0 copy-done.2
  1256.4 0.7 fusion.2
  1257.1 0.0 collective-permute-done.3
  1257.1 0.0 copy-done.3
  1257.1 0.6 fusion.3
Async XLA Ops:
  1209.1 47.9 %collective-permute-start.3 = (f32[32,512]{1,0:T(8,128)}, f32[32,512]{1,0:T(8,128)S(1)}, u32[]{:S(2)}, u32[]{:S(2)}) collective-permute-start(f32[32,512]{1,0:T(8,128)} %get-tuple-element.26), channel_id=1, source_target_pairs={{0,2},{2,0},{1,3},{3,1},{4,6},{6,4},{5,7},{7,5}} | collective-permute-start | bytes 196616 | tf_op jit(solution)/shard_map/ppermute | solution.py:473
  1211.1 45.2 %collective-permute-start.2 = (f32[96,512]{1,0:T(8,128)}, f32[96,512]{1,0:T(8,128)S(1)}, u32[]{:S(2)}, u32[]{:S(2)}) collective-permute-start(f32[96,512]{1,0:T(8,128)} %get-tuple-element.24), channel_id=1, source_target_pairs={{0,2},{2,0},{1,3},{3,1},{4,6},{6,4},{5,7},{7,5}} | collective-permute-start | bytes 589832 | tf_op jit(solution)/shard_map/ppermute | solution.py:473
  1211.2 43.2 %collective-permute-start.1 = (f32[384,512]{1,0:T(8,128)}, f32[384,512]{1,0:T(8,128)}, u32[]{:S(2)}, u32[]{:S(2)}) collective-permute-start(f32[384,512]{1,0:T(8,128)} %get-tuple-element.22), channel_id=1, source_target_pairs={{0,2},{2,0},{1,3},{3,1},{4,6},{6,4},{5,7},{7,5}} | collective-permute-start | bytes 2359304 | tf_op jit(solution)/shard_map/ppermute | solution.py:473
  1213.2 40.3 %collective-permute-start = (f32[512,512]{1,0:T(8,128)}, f32[512,512]{1,0:T(8,128)S(1)}, u32[]{:S(2)}, u32[]{:S(2)}) collective-permute-start(f32[512,512]{1,0:T(8,128)} %get-tuple-element.20), channel_id=1, source_target_pairs={{0,2},{2,0},{1,3},{3,1},{4,6},{6,4},{5,7},{7,5}} | collective-permute-start | bytes 3145736 | tf_op jit(solution)/shard_map/ppermute | solution.py:473
  1213.2 40.2 %copy-start = (f32[512,512]{1,0:T(8,128)S(1)}, f32[512,512]{1,0:T(8,128)}, u32[]{:S(2)}) copy-start(f32[512,512]{1,0:T(8,128)} %get-tuple-element.19) | copy-start | bytes 3145732
  1213.2 41.2 %copy-start.1 = (f32[384,512]{1,0:T(8,128)S(1)}, f32[384,512]{1,0:T(8,128)}, u32[]{:S(2)}) copy-start(f32[384,512]{1,0:T(8,128)} %get-tuple-element.21) | copy-start | bytes 2359300
  1213.2 43.2 %copy-start.2 = (f32[96,512]{1,0:T(8,128)S(1)}, f32[96,512]{1,0:T(8,128)}, u32[]{:S(2)}) copy-start(f32[96,512]{1,0:T(8,128)} %get-tuple-element.23) | copy-start | bytes 589828
  1213.2 43.9 %copy-start.3 = (f32[32,512]{1,0:T(8,128)S(1)}, f32[32,512]{1,0:T(8,128)}, u32[]{:S(2)}) copy-start(f32[32,512]{1,0:T(8,128)} %get-tuple-element.25) | copy-start | bytes 196612
